TPU v7x, 16 devices: a whole 2x2x2 slice. The times are simulated.
16 devices in a mesh: row: 4 (over z, y), col: 4 (over x, core).
Axes of the slice: x: 2, y: 2, z: 2, core: 2. Of those that a mesh axis runs over, the one named last changes fastest.
Arguments:
- v_mat: float32 [8192, 8192], P('row', 'col')
- t_fac: float32 [128, 64, 64], P('col')
- z_vec: float32 [8192, 1024], P(None, ('col', 'row'))
Outputs:
- output: float32 [8192, 1024], P('row', 'col')
All inputs are finite; a program needn't handle non-finite values.
Results may differ from a plain program's by a relative error of at most 0.001.
Values sent between devices are 32-bit elements.
A program may use at most 1 GiB of HBM per device.

v0:
```python
import jax
import jax.numpy as jnp
from jax import lax
from jax.sharding import PartitionSpec as P

FULL_PREC = lax.Precision.HIGHEST


def solution(mesh):
    col_shards = mesh.shape['col']

    def local_body(v_loc, t_loc, z_loc):
        panel_width = t_loc.shape[1]
        local_panels = t_loc.shape[0]
        num_panels = local_panels * col_shards
        my_col = lax.axis_index('col')
        t_all = lax.all_gather(t_loc, 'col', axis=0, tiled=True)
        x_loc = lax.all_to_all(z_loc, 'row', 0, 1, tiled=True)

        def panel_step(step_idx, x_cur):
            panel_idx = num_panels - 1 - step_idx
            owner_col = panel_idx % col_shards
            loc_slot = panel_idx // col_shards
            v_blk = lax.dynamic_slice_in_dim(v_loc, loc_slot * panel_width, panel_width, axis=1)
            v_pan = lax.psum(jnp.where(my_col == owner_col, v_blk, 0.0), 'col')
            t_pan = lax.dynamic_index_in_dim(t_all, owner_col * local_panels + loc_slot, axis=0, keepdims=False)
            w_part = jnp.einsum('nb,nk->bk', v_pan, x_cur, preferred_element_type=jnp.float32, precision=FULL_PREC)
            w_full = lax.psum(w_part, 'row')
            y_blk = jnp.dot(t_pan, w_full, preferred_element_type=jnp.float32, precision=FULL_PREC)
            return x_cur - jnp.dot(v_pan, y_blk, preferred_element_type=jnp.float32, precision=FULL_PREC)

        return lax.fori_loop(0, num_panels, panel_step, x_loc)

    return jax.shard_map(local_body, mesh=mesh,
                         in_specs=(P('row', 'col'), P('col', None, None), P(None, ('col', 'row'))),
                         out_specs=P('row', 'col'), check_vma=False)
```

profile of v0, /device:TPU:0, one launch (start us, length us, event | category | flops | bytes accessed | tf_op | source)
XLA Modules:
  0.0 10007.9 jit_solution(3610318477535031365)
XLA Ops:
  44.1 9955.6 %while.15 = (s32[]{:T(128)}, f32[2048,256]{1,0:T(8,128)S(1)}, s32[]{:T(128)}, f32[2048,2048]{1,0:T(8,128)}, f32[128,64,64]{2,1,0:T(8,128)}, /*index=5*/s32[]{:T(...) while((s32[]{:T(128)}, f32[2048,256]{1,0:T(8,128)S(1)}, ...), condition=%wide.region_3.4_spmd, body=%wide.region_0.3_spmd.sunk | while | flops 818692096 | bytes 15368770 | solution.py:32
  472.4 34.5 all-reduce.5.cloned.1.call-done
  1405.0 34.5 all-reduce.5.cloned.1.call-done
  1638.8 34.5 all-reduce.5.cloned.1.call-done
  1949.9 34.5 all-reduce.5.cloned.1.call-done
  2572.5 34.5 all-reduce.5.cloned.1.call-done
  2650.4 34.5 all-reduce.5.cloned.1.call-done
  3816.3 34.5 all-reduce.5.cloned.1.call-done
  4361.2 34.5 all-reduce.5.cloned.1.call-done
  4828.2 34.5 all-reduce.5.cloned.1.call-done
  5139.4 34.5 all-reduce.5.cloned.1.call-done
  5916.2 34.5 all-reduce.5.cloned.1.call-done
  6460.9 34.5 all-reduce.5.cloned.1.call-done
  7161.3 34.5 all-reduce.5.cloned.1.call-done
  7395.1 34.5 all-reduce.5.cloned.1.call-done
  7551.0 34.5 all-reduce.5.cloned.1.call-done
  7706.5 34.5 all-reduce.5.cloned.1.call-done
  7784.4 34.5 all-reduce.5.cloned.1.call-done
  7862.4 34.5 all-reduce.5.cloned.1.call-done
  8095.8 34.5 all-reduce.5.cloned.1.call-done
  8173.4 34.5 all-reduce.5.cloned.1.call-done
  8796.3 34.5 all-reduce.5.cloned.1.call-done
  9184.7 34.5 all-reduce.5.cloned.1.call-done
  9340.0 34.5 all-reduce.5.cloned.1.call-done
  (1524 shorter events, 9184.5 us)
Async XLA Ops:
  46.7 71.7 all-reduce.5.cloned.1.call-start
  280.0 71.6 all-reduce.5.cloned.1.call-start
  1056.8 71.6 all-reduce.5.cloned.1.call-start
  1290.3 71.6 all-reduce.5.cloned.1.call-start
  1523.8 71.6 all-reduce.5.cloned.1.call-start
  2146.6 71.6 all-reduce.5.cloned.1.call-start
  2380.1 71.6 all-reduce.5.cloned.1.call-start
  3079.7 71.6 all-reduce.5.cloned.1.call-start
  3623.6 71.6 all-reduce.5.cloned.1.call-start
  3701.6 71.6 all-reduce.5.cloned.1.call-start
  4246.2 71.6 all-reduce.5.cloned.1.call-start
  4480.0 71.6 all-reduce.5.cloned.1.call-start
  4713.5 71.6 all-reduce.5.cloned.1.call-start
  4947.0 71.6 all-reduce.5.cloned.1.call-start
  5723.9 71.6 all-reduce.5.cloned.1.call-start
  6346.2 71.6 all-reduce.5.cloned.1.call-start
  6813.1 71.6 all-reduce.5.cloned.1.call-start
  7280.1 71.6 all-reduce.5.cloned.1.call-start
  7980.8 71.6 all-reduce.5.cloned.1.call-start
  8292.2 71.6 all-reduce.5.cloned.1.call-start
  8447.8 71.6 all-reduce.5.cloned.1.call-start
  8525.7 71.6 all-reduce.5.cloned.1.call-start
  9070.0 71.6 all-reduce.5.cloned.1.call-start
  9846.9 71.6 all-reduce.5.cloned.1.call-start
  (364 other events, 17116.8 us)
Sparse Core Ops, SparseCore 0:
  8.9 35.2 all-gather.1
  472.5 34.3 all-reduce.4
  1405.2 34.3 all-reduce.4
  1639.0 34.3 all-reduce.4
  1950.0 34.3 all-reduce.4
  2572.6 34.3 all-reduce.4
  2650.5 34.3 all-reduce.4
  3816.4 34.3 all-reduce.4
  4361.3 34.3 all-reduce.4
  4828.3 34.3 all-reduce.4
  5139.5 34.3 all-reduce.4
  5916.4 34.3 all-reduce.4
  6461.0 34.3 all-reduce.4
  7161.4 34.3 all-reduce.4
  7395.2 34.3 all-reduce.4
  7551.1 34.3 all-reduce.4
  7706.6 34.3 all-reduce.4
  7784.6 34.3 all-reduce.4
  7862.5 34.3 all-reduce.4
  8095.9 34.3 all-reduce.4
  8173.5 34.3 all-reduce.4
  8796.4 34.3 all-reduce.4
  9184.8 34.3 all-reduce.4
  9340.1 34.3 all-reduce.4
  (233 shorter events, 7771.4 us)
where the time goes:
time: 10000 us
  waiting for transfers between devices  8670 us (87%)
  matrix products  960 us (10%)
  other arithmetic  325 us (3%)
    psum x128, waiting for transfers between devices, panel_step(): w_full = lax.psum(w_part, 'row')  4420 us
    psum x128, waiting for transfers between devices, panel_step(): v_pan = lax.psum(jnp.where(my_col == owner_col, v_blk, 0.0), 'col')  4220 us
    dot_general x128, matrix products, panel_step(): jnp.einsum('nb,nk->bk', v_pan, x_cur, preferred_element_type=jnp.float32,...  494 us
    dot_general x128, matrix products, panel_step(): jnp.dot(v_pan, y_blk, preferred_element_type=jnp.float32, precision=FULL_...  331 us
    select_n x128, other arithmetic, panel_step(): v_pan = lax.psum(jnp.where(my_col == owner_col, v_blk, 0.0), 'col')  325 us
  transfers between devices with their start and end apart: 258, of which 258 were waited for; matrix products, arithmetic and copies ran while one was open for 0% of the time, Pallas kernels for 0%

commit v1 on v0

v1 whole, which is shorter than its diff:
```python
import jax
import jax.numpy as jnp
from jax import lax
from jax.experimental import pallas as pl
from jax.experimental.pallas import tpu as pltpu
from jax.sharding import PartitionSpec as P

F32 = jnp.float32
MESH = pl.DeviceIdType.MESH
TILE = 256
AHEAD = 8


def dot(a, b, ca, cb):
    return lax.dot_general(a, b, (((ca,), (cb,)), ((), ())), preferred_element_type=F32,
                           precision=lax.Precision.HIGHEST)


def make_kernel(rows, blocks):
    def tiles_of(h):
        return (blocks + 1 - h) // 2

    def tiles_before(h):
        k = blocks - 1 - h
        return ((k + 1) // 2) * ((k + 2) // 2)

    def body(v_hbm, t_hbm, z_hbm, x_ref, vbuf, vs, tall, zbuf, wacc, r1, ws, r2, y_ref, gacc, gr1, gs, gr2, tbuf, gab,
             vx_s, vsib_s, vfwd_s, vloc_s, v_r, tx_s, txc_s, tsib_s, tloc_s, t_r, z_s, zloc_s, z_r,
             p1_s, p1_r, p2_s, p2_r, g1_s, g1_r, g2_s, g2_r, d_s, d_r):
        r = lax.axis_index("row")
        c = lax.axis_index("col")
        core = c % 2
        cx, csib, cxc = (c + 2) % 4, c + 1 - 2 * core, 3 - c
        ry, rz, rd = r + 1 - 2 * (r % 2), (r + 2) % 4, 3 - r
        dev_x, dev_sib, dev_xc = (r, cx), (r, csib), (r, cxc)
        dev_y, dev_z, dev_d = (ry, c), (rz, c), (rd, c)

        def remote(src, dst, ss, rs, dev):
            return pltpu.make_async_remote_copy(src, dst, ss, rs, device_id=dev, device_id_type=MESH)

        barrier = pltpu.get_barrier_semaphore()
        for dev in (dev_x, dev_sib, dev_xc, dev_y, dev_z, dev_d):
            pl.semaphore_signal(barrier, 1, device_id=dev, device_id_type=MESH)
        pl.semaphore_wait(barrier, 6)

        def v_src(hh):
            n = TILE * tiles_of(hh)
            return v_hbm.at[pl.ds(rows - n, n), pl.ds(hh * 128, 128)]

        def v_dst(slot, hh):
            return vbuf.at[slot, pl.ds(TILE * tiles_before(hh), TILE * tiles_of(hh)), :]

        def v_x(hh):
            return remote(v_src(hh), v_dst(c, hh), vx_s.at[hh], v_r.at[c, hh], dev_x)

        def v_sib(hh):
            return remote(v_src(hh), v_dst(c, hh), vsib_s.at[hh], v_r.at[c, hh], dev_sib)

        def v_fwd(hh):
            return remote(v_dst(cx, hh), v_dst(cx, hh), vfwd_s.at[hh], v_r.at[cx, hh], dev_sib)

        def v_loc(hh):
            return pltpu.make_async_copy(v_src(hh), v_dst(c, hh), vloc_s.at[hh])

        def v_arrive(slot, hh):
            return remote(v_src(hh), v_dst(slot, hh), vx_s.at[hh], v_r.at[slot, hh], dev_x)

        def t_copies(h):
            return (remote(t_hbm.at[h, core], tall.at[c, h], tx_s.at[h], t_r.at[c, h], dev_x),
                    remote(t_hbm.at[h, 1 - core], tall.at[c, h], txc_s.at[h], t_r.at[c, h], dev_xc),
                    remote(t_hbm.at[h, 1 - core], tall.at[c, h], tsib_s.at[h], t_r.at[c, h], dev_sib))

        def t_loc(h):
            return pltpu.make_async_copy(t_hbm.at[h, core], tall.at[c, h], tloc_s.at[h])

        def t_arrive(slot, h):
            return remote(t_hbm.at[h, core], tall.at[slot, h], tx_s.at[h], t_r.at[slot, h], dev_x)

        def issue_v(hh):
            for cp in t_copies(hh):
                cp.start()
            t_loc(hh).start()
            v_x(hh).start()
            v_loc(hh).start()
            v_sib(hh).start()

        def collect_v(hh):
            v_arrive(cx, hh).wait_recv()
            v_fwd(hh).start()
            v_loc(hh).wait()
            v_arrive(csib, hh).wait_recv()
            v_arrive(cxc, hh).wait_recv()
            t_loc(hh).wait()
            for slot in (cx, csib, cxc):
                t_arrive(slot, hh).wait_recv()

        def z_copies(t):
            out = []
            for i, dev in enumerate((dev_y, dev_z, dev_d)):
                src = z_hbm.at[pl.ds(rows * dev[0] + TILE * t, TILE), :]
                out.append(remote(src, zbuf.at[r, pl.ds(TILE * t, TILE), :], z_s.at[i, t], z_r.at[r, t], dev))
            return out

        def z_loc(t):
            src = z_hbm.at[pl.ds(rows * r + TILE * t, TILE), :]
            return pltpu.make_async_copy(src, zbuf.at[r, pl.ds(TILE * t, TILE), :], zloc_s.at[t])

        def issue_z(t):
            for cp in z_copies(t):
                cp.start()
            z_loc(t).start()

        def collect_z(t):
            z_loc(t).wait()
            for src_r in (ry, rz, rd):
                dst = zbuf.at[src_r, pl.ds(TILE * t, TILE), :]
                remote(z_hbm.at[pl.ds(0, TILE), :], dst, z_s.at[0, t], z_r.at[src_r, t], dev_y).wait_recv()
            s = pl.ds(TILE * t, TILE)
            for i in range(4):
                x_ref[s, 64 * i:64 * i + 64] = zbuf[i, s, :]

        def steps(half):
            return (dev_y, dev_z) if half == 0 else (dev_z, dev_y)

        def w_p1(p, half):
            s = pl.ds(128 * half, 128)
            return remote(wacc.at[p, s], r1.at[p, s], p1_s.at[p, half], p1_r.at[p, half], steps(half)[0])

        def w_p2(p, half):
            s = pl.ds(128 * half, 128)
            return remote(ws.at[p, s], r2.at[p, s], p2_s.at[p, half], p2_r.at[p, half], steps(half)[1])

        def g_p1(half):
            s = pl.ds(224 * half, 224)
            return remote(gacc.at[s], gr1.at[s], g1_s.at[half], g1_r.at[half], steps(half)[0])

        def g_p2(half):
            s = pl.ds(224 * half, 224)
            return remote(gs.at[s], gr2.at[s], g2_s.at[half], g2_r.at[half], steps(half)[1])

        def over_tiles(n, fn):
            def pair(t, _):
                fn(2 * TILE * t, 2 * TILE)
                return 0
            lax.fori_loop(0, n // 2, pair, 0)

            @pl.when(n % 2 == 1)
            def _():
                fn(TILE * (n - 1), TILE)

        def regroup(h, slot):
            base = TILE * tiles_before(h)

            def one(t, _):
                s = pl.ds(pl.multiple_of(base + TILE * t, TILE), TILE)
                d = pl.ds(pl.multiple_of(TILE * t, TILE), TILE)
                for i in range(2):
                    a, b = vbuf[2 * i, s, :], vbuf[2 * i + 1, s, :]
                    low = lax.broadcasted_iota(jnp.int32, a.shape, 1) < 64
                    ar, br = pltpu.roll(a, 64, 1), pltpu.roll(b, 64, 1)
                    vs[slot, d, 128 * i:128 * i + 128] = jnp.where(low, a, br)
                    vs[slot, d, 256 + 128 * i:256 + 128 * i + 128] = jnp.where(low, ar, b)
                return 0
            lax.fori_loop(0, tiles_of(h), one, 0)

        def gram(h, slot):
            gacc[...] = jnp.zeros_like(gacc)
            y_ref[...] = jnp.zeros_like(y_ref)

            def one(off, n):
                s = pl.ds(pl.multiple_of(off, TILE), n)
                own = vs[slot, s, pl.ds(pl.multiple_of(256 * core, 256), 256)]
                y_ref[0:256, :] += dot(own, own, 0, 0)
                half = vs[slot, s, pl.ds(pl.multiple_of(256 + 128 * core, 128), 128)]
                gacc[0:256, :] += dot(vs[slot, s, 0:256], half, 0, 0)
            over_tiles(tiles_of(h), one)
            gacc[256:384, :] = y_ref[0:128, 128:256]
            gacc[384:448, 0:64] = y_ref[0:64, 64:128]
            gacc[384:448, 64:128] = y_ref[128:192, 192:256]

        def act_g():
            for half in range(2):
                g_p1(half).wait()
            gs[...] = gacc[...] + gr1[...]
            for half in range(2):
                g_p2(half).start()

        def share(slot):
            return (remote(tbuf.at[slot, core], tbuf.at[slot, core], d_s.at[slot, 0], d_r.at[slot, 0], dev_sib),
                    remote(gab.at[slot, core], gab.at[slot, core], d_s.at[slot, 1], d_r.at[slot, 1], dev_sib))

        def shared(slot):
            return (remote(tbuf.at[slot, 1 - core], tbuf.at[slot, 1 - core], d_s.at[slot, 0], d_r.at[slot, 0], dev_sib),
                    remote(gab.at[slot, 1 - core], gab.at[slot, 1 - core], d_s.at[slot, 1], d_r.at[slot, 1], dev_sib))

        def merge(h, slot):
            for half in range(2):
                g_p2(half).wait()
            g = gs[...] + gr2[...]
            gab[slot, core] = g[0:256]
            zero = jnp.zeros((64, 64), F32)

            def diag(a, b):
                return jnp.concatenate([jnp.concatenate([a, zero], 1), jnp.concatenate([zero, b], 1)], 0)
            t0, t1, t2, t3 = (tall[i, h] for i in range(4))
            low = g[384:448]
            off = dot(diag(low[:, 0:64], low[:, 64:128]), diag(t1, t3), 1, 0)
            off = -dot(diag(t0, t2), off, 1, 0)
            ta = jnp.concatenate([jnp.concatenate([t0, off[0:64, 0:64]], 1), jnp.concatenate([zero, t1], 1)], 0)
            tb = jnp.concatenate([jnp.concatenate([t2, off[64:128, 64:128]], 1), jnp.concatenate([zero, t3], 1)], 0)
            cross = -dot(ta, dot(g[256:384], tb, 1, 0), 1, 0)
            tbuf[slot, core, 0:128, 0:128] = ta
            tbuf[slot, core, 0:128, 128:256] = cross
            tbuf[slot, core, 128:256, 0:128] = jnp.zeros((128, 128), F32)
            tbuf[slot, core, 128:256, 128:256] = tb

        def product(h, slot, p):
            wacc[p] = jnp.zeros((256, 256), F32)
            row0 = rows - TILE * tiles_of(h)

            def one(off, n):
                s = pl.ds(pl.multiple_of(off, TILE), n)
                sx = pl.ds(pl.multiple_of(row0 + off, TILE), n)
                wacc[p] += dot(vs[slot, s, 256 * p:256 * p + 256], x_ref[sx, :], 0, 0)
            over_tiles(tiles_of(h), one)
            for half in range(2):
                w_p1(p, half).start()

        def act_w(p):
            for half in range(2):
                w_p1(p, half).wait()
            ws[p] = wacc[p] + r1[p]
            for half in range(2):
                w_p2(p, half).start()

        def reduced(p):
            for half in range(2):
                w_p2(p, half).wait()
            return ws[p] + r2[p]

        def update(h, slot):
            row0 = rows - TILE * tiles_of(h)

            def one(off, n):
                s = pl.ds(pl.multiple_of(off, TILE), n)
                sx = pl.ds(pl.multiple_of(row0 + off, TILE), n)
                x_ref[sx, :] -= dot(vs[slot, s, :], y_ref[...], 1, 0)
            over_tiles(tiles_of(h), one)

        last = blocks - 1
        for t in (rows // TILE - 1, rows // TILE - 2):
            issue_z(t)
        for hh in range(last, last - AHEAD, -1):
            issue_v(hh)
        collect_v(last)
        regroup(last, last % 2)
        gram(last, last % 2)
        for half in range(2):
            g_p1(half).start()
        act_g()
        merge(last, last % 2)
        for cp in share(last % 2):
            cp.start()

        def block_step(i, _):
            h = last - i
            slot = h % 2
            nslot = 1 - slot

            @pl.when(slot == 1)
            def _():
                collect_z((h - 1) // 2)

            @pl.when(jnp.logical_and(slot == 1, h >= 5))
            def _():
                issue_z((h - 1) // 2 - 2)

            product(h, slot, 1)
            product(h, slot, 0)
            for hh in range(blocks - AHEAD):
                @pl.when(h == hh + AHEAD)
                def _():
                    issue_v(hh)
            for hh in range(blocks - 1):
                @pl.when(h - 1 == hh)
                def _():
                    collect_v(hh)

            @pl.when(h > 0)
            def _():
                regroup(h - 1, nslot)
                gram(h - 1, nslot)
                for half in range(2):
                    g_p1(half).start()
            act_w(1)
            act_w(0)

            @pl.when(h > 0)
            def _():
                act_g()
            for cp in share(slot):
                cp.wait_send()
            for cp in shared(slot):
                cp.wait_recv()
            yb = dot(tbuf[slot, 1], reduced(1), 1, 0)
            y_ref[256:512, :] = yb
            wa = reduced(0) - dot(gab[slot, 0], yb[0:128], 1, 0) - dot(gab[slot, 1], yb[128:256], 1, 0)
            y_ref[0:256, :] = dot(tbuf[slot, 0], wa, 1, 0)

            @pl.when(h > 0)
            def _():
                merge(h - 1, nslot)
                for cp in share(nslot):
                    cp.start()
            update(h, slot)
            return 0

        lax.fori_loop(0, blocks, block_step, 0)
        for hh in range(blocks):
            v_x(hh).wait_send()
            v_sib(hh).wait_send()
            v_fwd(hh).wait_send()
            for cp in t_copies(hh):
                cp.wait_send()
        for t in range(rows // TILE):
            for cp in z_copies(t):
                cp.wait_send()

    return body


def solution(mesh):
    def local(v_loc, t_loc, z_loc):
        rows, cols = v_loc.shape
        blocks = cols // 128
        t_loc = t_loc.reshape(blocks, 2, 64, 64)
        tiles = ((blocks + 1) // 2) * ((blocks + 2) // 2)
        dma = pltpu.SemaphoreType.DMA
        hbm = pl.BlockSpec(memory_space=pl.ANY)
        return pl.pallas_call(
            make_kernel(rows, blocks),
            out_shape=jax.ShapeDtypeStruct((rows, 256), F32),
            in_specs=[hbm] * 3,
            out_specs=pl.BlockSpec(memory_space=pltpu.VMEM),
            scratch_shapes=[
                pltpu.VMEM((4, TILE * tiles, 128), F32),
                pltpu.VMEM((2, rows, 512), F32),
                pltpu.VMEM((4, blocks, 64, 64), F32),
                pltpu.VMEM((4, rows, 64), F32),
                pltpu.VMEM((2, 256, 256), F32), pltpu.VMEM((2, 256, 256), F32),
                pltpu.VMEM((2, 256, 256), F32), pltpu.VMEM((2, 256, 256), F32),
                pltpu.VMEM((512, 256), F32),
                pltpu.VMEM((448, 128), F32), pltpu.VMEM((448, 128), F32),
                pltpu.VMEM((448, 128), F32), pltpu.VMEM((448, 128), F32),
                pltpu.VMEM((2, 2, 256, 256), F32),
                pltpu.VMEM((2, 2, 256, 128), F32),
                dma((blocks,)), dma((blocks,)), dma((blocks,)), dma((blocks,)), dma((4, blocks)),
                dma((blocks,)), dma((blocks,)), dma((blocks,)), dma((blocks,)), dma((4, blocks)),
                dma((3, rows // TILE)), dma((rows // TILE,)), dma((4, rows // TILE)),
                dma((2, 2)), dma((2, 2)), dma((2, 2)), dma((2, 2)),
                dma((2,)), dma((2,)), dma((2,)), dma((2,)),
                dma((2, 2)), dma((2, 2)),
            ],
            compiler_params=pltpu.CompilerParams(collective_id=0, has_side_effects=True,
                                                 vmem_limit_bytes=67043328),
        )(v_loc, t_loc, z_loc)

    return jax.shard_map(local, mesh=mesh,
                         in_specs=(P('row', 'col'), P('col', None, None), P(None, ('col', 'row'))),
                         out_specs=P('row', 'col'), check_vma=False)
```

time: 10000 us -> 462 us (0.05)
  waiting for transfers between devices: 8670 us -> 0 us
  matrix products: 960 us -> 0 us
  Pallas kernels: 0 us -> 455 us
  other arithmetic: 325 us -> 0 us
    psum x256 -> x0, waiting for transfers between devices: 8640 us -> none  [the longest x128 4420 us: panel_step(): w_full = lax.psum(w_part, 'row')]
    dot_general x384 -> x0, matrix products: 960 us -> none  [the longest x128 494 us: panel_step(): jnp.einsum('nb,nk->bk', v_pan, x_cur, preferred_element_type=jnp.float32,...]
    pallas_call x0 -> x1, Pallas kernels: none -> 455 us  [local(): pl.pallas_call(make_kernel(rows, blocks), out_shape=jax.ShapeDtypeStruct(...]
    select_n x128 -> x0, other arithmetic: 325 us -> none  [panel_step(): v_pan = lax.psum(jnp.where(my_col == owner_col, v_blk, 0.0), 'col')]
  transfers between devices with their start and end apart: 258 -> 0, of which waited for: 258 -> 0; matrix products, arithmetic and copies ran while one was open for 0% -> 0% of each run, Pallas kernels for 0% -> 0%
where the time goes in v1:
time: 462 us
  Pallas kernels  455 us (98%)
  local copies, waits for them, and re-layouts  6.81 us (1%)
    pallas_call x1, Pallas kernels, local(): pl.pallas_call(make_kernel(rows, blocks), out_shape=jax.ShapeDtypeStruct(...  455 us

profile of v1, /device:TPU:0, one launch (start us, length us, event | category | flops | bytes accessed | tf_op | source)
XLA Modules:
  0.0 461.5 jit_solution(2421238330112938093)
XLA Ops:
  0.0 3.8 copy.4.z_hbm
  3.8 454.7 %shard_map.37 = f32[2048,256]{1,0:T(8,128)} custom-call(f32[2048,2048]{1,0:T(8,128)} %v_hbm.1, f32[16,2,64,64]{3,2,1,0:T(8,128)} %bitcast.1, f32[8192,64]{1,0:T(8,128)} %copy.4.z_hbm), custom_call_target="tpu_custom_call" | custom-call | tf_op jit(solution)/shard_map/pallas_call | solution.py:340
  458.5 3.0 copy.6

commit v2 on v1

--- a/solution.py
+++ b/solution.py
@@ -9,6 +9,7 @@
 MESH = pl.DeviceIdType.MESH
 TILE = 256
 AHEAD = 8
+Z_AHEAD = 4
 
 
 def dot(a, b, ca, cb):
@@ -84,9 +85,11 @@
             v_loc(hh).start()
             v_sib(hh).start()
 
-        def collect_v(hh):
+        def forward_v(hh):
             v_arrive(cx, hh).wait_recv()
             v_fwd(hh).start()
+
+        def collect_v(hh):
             v_loc(hh).wait()
             v_arrive(csib, hh).wait_recv()
             v_arrive(cxc, hh).wait_recv()
@@ -94,16 +97,17 @@
             for slot in (cx, csib, cxc):
                 t_arrive(slot, hh).wait_recv()
 
+        def z_src(to, t):
+            return z_hbm.at[:, pl.ds(pl.multiple_of(rows * to + TILE * t, TILE), TILE)]
+
         def z_copies(t):
             out = []
             for i, dev in enumerate((dev_y, dev_z, dev_d)):
-                src = z_hbm.at[pl.ds(rows * dev[0] + TILE * t, TILE), :]
-                out.append(remote(src, zbuf.at[r, pl.ds(TILE * t, TILE), :], z_s.at[i, t], z_r.at[r, t], dev))
+                out.append(remote(z_src(dev[0], t), zbuf.at[t, r], z_s.at[i, t], z_r.at[r, t], dev))
             return out
 
         def z_loc(t):
-            src = z_hbm.at[pl.ds(rows * r + TILE * t, TILE), :]
-            return pltpu.make_async_copy(src, zbuf.at[r, pl.ds(TILE * t, TILE), :], zloc_s.at[t])
+            return pltpu.make_async_copy(z_src(r, t), zbuf.at[t, r], zloc_s.at[t])
 
         def issue_z(t):
             for cp in z_copies(t):
@@ -113,11 +117,8 @@
         def collect_z(t):
             z_loc(t).wait()
             for src_r in (ry, rz, rd):
-                dst = zbuf.at[src_r, pl.ds(TILE * t, TILE), :]
-                remote(z_hbm.at[pl.ds(0, TILE), :], dst, z_s.at[0, t], z_r.at[src_r, t], dev_y).wait_recv()
-            s = pl.ds(TILE * t, TILE)
-            for i in range(4):
-                x_ref[s, 64 * i:64 * i + 64] = zbuf[i, s, :]
+                remote(z_src(r, t), zbuf.at[t, src_r], z_s.at[0, t], z_r.at[src_r, t], dev_y).wait_recv()
+            x_ref[pl.ds(pl.multiple_of(TILE * t, TILE), TILE), :] = zbuf[t].reshape(256, TILE).T
 
         def steps(half):
             return (dev_y, dev_z) if half == 0 else (dev_z, dev_y)
@@ -248,19 +249,21 @@
             over_tiles(tiles_of(h), one)
 
         last = blocks - 1
-        for t in (rows // TILE - 1, rows // TILE - 2):
+        top = rows // TILE - 1
+        issue_v(last)
+        issue_z(top)
+        for hh in range(last - 1, last - AHEAD, -1):
+            issue_v(hh)
+        for t in range(top - 1, top - Z_AHEAD, -1):
             issue_z(t)
-        for hh in range(last, last - AHEAD, -1):
-            issue_v(hh)
+        forward_v(last)
+        forward_v(last - 1)
         collect_v(last)
         regroup(last, last % 2)
         gram(last, last % 2)
         for half in range(2):
             g_p1(half).start()
         act_g()
-        merge(last, last % 2)
-        for cp in share(last % 2):
-            cp.start()
 
         def block_step(i, _):
             h = last - i
@@ -271,12 +274,16 @@
             def _():
                 collect_z((h - 1) // 2)
 
-            @pl.when(jnp.logical_and(slot == 1, h >= 5))
-            def _():
-                issue_z((h - 1) // 2 - 2)
-
             product(h, slot, 1)
             product(h, slot, 0)
+            merge(h, slot)
+            for cp in share(slot):
+                cp.start()
+            act_w(1)
+            for hh in range(blocks - 2):
+                @pl.when(h - 2 == hh)
+                def _():
+                    forward_v(hh)
             for hh in range(blocks - AHEAD):
                 @pl.when(h == hh + AHEAD)
                 def _():
@@ -289,15 +296,13 @@
             @pl.when(h > 0)
             def _():
                 regroup(h - 1, nslot)
+            act_w(0)
+
+            @pl.when(h > 0)
+            def _():
                 gram(h - 1, nslot)
                 for half in range(2):
                     g_p1(half).start()
-            act_w(1)
-            act_w(0)
-
-            @pl.when(h > 0)
-            def _():
-                act_g()
             for cp in share(slot):
                 cp.wait_send()
             for cp in shared(slot):
@@ -307,12 +312,14 @@
             wa = reduced(0) - dot(gab[slot, 0], yb[0:128], 1, 0) - dot(gab[slot, 1], yb[128:256], 1, 0)
             y_ref[0:256, :] = dot(tbuf[slot, 0], wa, 1, 0)
 
+            @pl.when(jnp.logical_and(slot == 1, h >= 2 * Z_AHEAD + 1))
+            def _():
+                issue_z((h - 1) // 2 - Z_AHEAD)
+            update(h, slot)
+
             @pl.when(h > 0)
             def _():
-                merge(h - 1, nslot)
-                for cp in share(nslot):
-                    cp.start()
-            update(h, slot)
+                act_g()
             return 0
 
         lax.fori_loop(0, blocks, block_step, 0)
@@ -346,7 +353,7 @@
                 pltpu.VMEM((4, TILE * tiles, 128), F32),
                 pltpu.VMEM((2, rows, 512), F32),
                 pltpu.VMEM((4, blocks, 64, 64), F32),
-                pltpu.VMEM((4, rows, 64), F32),
+                pltpu.VMEM((rows // TILE, 4, 64, TILE), F32),
                 pltpu.VMEM((2, 256, 256), F32), pltpu.VMEM((2, 256, 256), F32),
                 pltpu.VMEM((2, 256, 256), F32), pltpu.VMEM((2, 256, 256), F32),
                 pltpu.VMEM((512, 256), F32),
@@ -363,7 +370,7 @@
             ],
             compiler_params=pltpu.CompilerParams(collective_id=0, has_side_effects=True,
                                                  vmem_limit_bytes=67043328),
-        )(v_loc, t_loc, z_loc)
+        )(v_loc, t_loc, z_loc.T)
 
     return jax.shard_map(local, mesh=mesh,
                          in_specs=(P('row', 'col'), P('col', None, None), P(None, ('col', 'row'))),

time: 462 us -> 336 us (0.73)
  Pallas kernels: 455 us -> 333 us
    pallas_call x1, Pallas kernels: 455 us -> 333 us  [local(): pl.pallas_call(make_kernel(rows, blocks), out_shape=jax.ShapeDtypeStruct(...]
where the time goes in v2:
time: 336 us
  Pallas kernels  333 us (99%)
    pallas_call x1, Pallas kernels, local(): pl.pallas_call(make_kernel(rows, blocks), out_shape=jax.ShapeDtypeStruct(...  333 us

profile of v2, /device:TPU:0, one launch (start us, length us, event | category | flops | bytes accessed | tf_op | source)
XLA Modules:
  0.0 336.0 jit_solution(6205300687018692466)
XLA Ops:
  0.0 333.0 %shard_map.37 = f32[2048,256]{1,0:T(8,128)} custom-call(f32[2048,2048]{1,0:T(8,128)} %v_hbm.1, f32[16,2,64,64]{3,2,1,0:T(8,128)} %bitcast.3, f32[64,8192]{1,0:T(8,128)} %bitcast.2), custom_call_target="tpu_custom_call" | custom-call | tf_op jit(solution)/shard_map/pallas_call | solution.py:347
  333.0 3.0 copy.5

commit v3 on v2

v3 whole, which is shorter than its diff:
```python
import jax
import jax.numpy as jnp
from jax import lax
from jax.experimental import pallas as pl
from jax.experimental.pallas import tpu as pltpu
from jax.sharding import PartitionSpec as P

F32 = jnp.float32
BF16 = jnp.bfloat16
MESH = pl.DeviceIdType.MESH
TILE = 256
AHEAD = 8
Z_START = 4
SWITCH = 10


def dot(a, b, ca, cb):
    return lax.dot_general(a, b, (((ca,), (cb,)), ((), ())), preferred_element_type=F32,
                           precision=lax.Precision.HIGHEST)


def split(a):
    a1 = a.astype(BF16)
    rest = a - a1.astype(F32)
    a2 = rest.astype(BF16)
    return a1, a2, (rest - a2.astype(F32)).astype(BF16)


def dot6(pairs, ca, cb):
    lhs, rhs = [], []
    for (a1, a2, a3), (b1, b2, b3) in pairs:
        lhs += [a3, a1, a2, a1, a2, a1]
        rhs += [b1, b3, b2, b2, b1, b1]
    return lax.dot_general(jnp.concatenate(lhs, ca), jnp.concatenate(rhs, cb), (((ca,), (cb,)), ((), ())),
                           preferred_element_type=F32)


def make_kernel(rows, blocks):
    def tiles_of(h):
        return (blocks + 1 - h) // 2

    def tiles_before(h):
        k = blocks - 1 - h
        return ((k + 1) // 2) * ((k + 2) // 2)

    area = TILE * tiles_before(-1)

    def body(v_hbm, t_hbm, z_hbm, o_ref, vbuf, vp, tall, xt, wacc, r1, ws, r2, yp, gkk, gacc, gr1, gs, gr2, tbuf, gab,
             nbuf, vx_s, vsib_s, vfwd_s, vloc_s, v_r, tx_s, txc_s, tsib_s, tloc_s, t_r, z_s, zloc_s, z_r,
             p1_s, p1_r, p2_s, p2_r, g1_s, g1_r, g2_s, g2_r, d_s, d_r):
        r = lax.axis_index("row")
        c = lax.axis_index("col")
        core = c % 2
        cx, csib, cxc = (c + 2) % 4, c + 1 - 2 * core, 3 - c
        ry, rz, rd = r + 1 - 2 * (r % 2), (r + 2) % 4, 3 - r
        dev_x, dev_sib, dev_xc = (r, cx), (r, csib), (r, cxc)
        dev_y, dev_z, dev_d = (ry, c), (rz, c), (rd, c)

        def remote(src, dst, ss, rs, dev):
            return pltpu.make_async_remote_copy(src, dst, ss, rs, device_id=dev, device_id_type=MESH)

        barrier = pltpu.get_barrier_semaphore()
        for dev in (dev_x, dev_sib, dev_xc, dev_y, dev_z, dev_d):
            pl.semaphore_signal(barrier, 1, device_id=dev, device_id_type=MESH)
        pl.semaphore_wait(barrier, 6)

        def v_src(hh):
            n = TILE * tiles_of(hh)
            return v_hbm.at[pl.ds(rows - n, n), pl.ds(hh * 128, 128)]

        def v_dst(rel, hh):
            return vbuf.at[pl.ds(area * (rel - 1) + TILE * tiles_before(hh), TILE * tiles_of(hh)), :]

        def v_x(hh):
            return remote(v_src(hh), v_dst(2, hh), vx_s.at[hh], v_r.at[1, hh], dev_x)

        def v_sib(hh):
            return remote(v_src(hh), v_dst(1, hh), vsib_s.at[hh], v_r.at[0, hh], dev_sib)

        def v_fwd(hh):
            return remote(v_dst(2, hh), v_dst(3, hh), vfwd_s.at[hh], v_r.at[2, hh], dev_sib)

        def v_loc(hh):
            dst = vbuf.at[pl.ds(3 * area + rows * (hh % 2), TILE * tiles_of(hh)), :]
            return pltpu.make_async_copy(v_src(hh), dst, vloc_s.at[hh])

        def v_arrive(rel, hh):
            return remote(v_src(hh), v_dst(rel, hh), vx_s.at[hh], v_r.at[rel - 1, hh], dev_x)

        def t_copies(h):
            return (remote(t_hbm.at[h, core], tall.at[c, h], tx_s.at[h], t_r.at[c, h], dev_x),
                    remote(t_hbm.at[h, 1 - core], tall.at[c, h], txc_s.at[h], t_r.at[c, h], dev_xc),
                    remote(t_hbm.at[h, 1 - core], tall.at[c, h], tsib_s.at[h], t_r.at[c, h], dev_sib))

        def t_loc(h):
            return pltpu.make_async_copy(t_hbm.at[h, core], tall.at[c, h], tloc_s.at[h])

        def t_arrive(slot, h):
            return remote(t_hbm.at[h, core], tall.at[slot, h], tx_s.at[h], t_r.at[slot, h], dev_x)

        def issue_v(hh):
            for cp in t_copies(hh):
                cp.start()
            t_loc(hh).start()
            v_x(hh).start()
            v_sib(hh).start()

        def forward_v(hh):
            v_arrive(2, hh).wait_recv()
            v_fwd(hh).start()

        def collect_v(hh):
            v_loc(hh).wait()
            v_arrive(1, hh).wait_recv()
            v_arrive(3, hh).wait_recv()
            t_loc(hh).wait()
            for slot in (cx, csib, cxc):
                t_arrive(slot, hh).wait_recv()

        def z_src(to, t):
            return z_hbm.at[:, pl.ds(pl.multiple_of(rows * to + TILE * t, TILE), TILE)]

        def z_dst(src_r, t):
            return xt.at[t, pl.ds(pl.multiple_of(64 * src_r, 64), 64), :]

        def z_copies(t):
            return [remote(z_src(dev[0], t), z_dst(r, t), z_s.at[i, t], z_r.at[r, t], dev)
                    for i, dev in enumerate((dev_y, dev_z, dev_d))]

        def z_loc(t):
            return pltpu.make_async_copy(z_src(r, t), z_dst(r, t), zloc_s.at[t])

        def issue_z(t):
            for cp in z_copies(t):
                cp.start()
            z_loc(t).start()

        def collect_z(t):
            z_loc(t).wait()
            for src_r in (ry, rz, rd):
                remote(z_src(r, t), z_dst(src_r, t), z_s.at[0, t], z_r.at[src_r, t], dev_y).wait_recv()

        def steps(half):
            return (dev_y, dev_z) if half == 0 else (dev_z, dev_y)

        def w_p1(p, half):
            s = pl.ds(128 * half, 128)
            return remote(wacc.at[p, s], r1.at[p, s], p1_s.at[p, half], p1_r.at[p, half], steps(half)[0])

        def w_p2(p, half):
            s = pl.ds(128 * half, 128)
            return remote(ws.at[p, s], r2.at[p, s], p2_s.at[p, half], p2_r.at[p, half], steps(half)[1])

        def g_p1(half):
            s = pl.ds(224 * half, 224)
            return remote(gacc.at[s], gr1.at[s], g1_s.at[half], g1_r.at[half], steps(half)[0])

        def g_p2(half):
            s = pl.ds(224 * half, 224)
            return remote(gs.at[s], gr2.at[s], g2_s.at[half], g2_r.at[half], steps(half)[1])

        def over_tiles(n, fn):
            def four(t, _):
                fn(4 * t, 4)
                return 0
            lax.fori_loop(0, n // 4, four, 0)

            @pl.when(n % 4 >= 2)
            def _():
                fn(4 * (n // 4), 2)

            @pl.when(n % 2 == 1)
            def _():
                fn(n - 1, 1)

        def prepare(h, slot):
            bases = []
            for i in range(4):
                rel = ((c // 2 + i // 2) % 2) * 2 + (c + i) % 2
                own = (3 - rel) // 3
                bases.append(own * (3 * area + rows * (h % 2)) + (1 - own) * (area * (rel - 1) + TILE * tiles_before(h)))

            def one(t, _):
                d = pl.ds(pl.multiple_of(TILE * t, TILE), TILE)
                for i in range(2):
                    a = vbuf[pl.ds(pl.multiple_of(bases[2 * i] + TILE * t, TILE), TILE), :]
                    b = vbuf[pl.ds(pl.multiple_of(bases[2 * i + 1] + TILE * t, TILE), TILE), :]
                    low = lax.broadcasted_iota(jnp.int32, a.shape, 1) < 64
                    ar, br = pltpu.roll(a, 64, 1), pltpu.roll(b, 64, 1)
                    for k, part in enumerate(split(jnp.where(low, a, br))):
                        vp[slot, k, d, 128 * i:128 * i + 128] = part
                    for k, part in enumerate(split(jnp.where(low, ar, b))):
                        vp[slot, k, d, 256 + 128 * i:256 + 128 * i + 128] = part
                return 0
            lax.fori_loop(0, tiles_of(h), one, 0)

        def parts(slot, t, lanes):
            s = pl.ds(pl.multiple_of(TILE * t, TILE), TILE)
            return tuple(vp[slot, k, s, lanes] for k in range(3))

        def gram(h, slot):
            gkk[...] = jnp.zeros_like(gkk)
            mine = pl.ds(pl.multiple_of(256 * core, 256), 256)
            half = pl.ds(pl.multiple_of(128 * core, 128), 128)

            def one(t, n):
                own = [parts(slot, t + u, mine) for u in range(n)]
                gkk[0:256, :] += dot6([(a, a) for a in own], 0, 0)
                gkk[256:384, :] += dot6([(parts(slot, t + u, half), parts(slot, t + u, pl.ds(256, 256)))
                                         for u in range(n)], 0, 0)
            over_tiles(tiles_of(h), one)
            gacc[0:128, :] = gkk[256:384, 0:128]
            gacc[128:256, :] = gkk[256:384, 128:256]
            gacc[256:384, :] = gkk[0:128, 128:256]
            gacc[384:448, 0:64] = gkk[0:64, 64:128]
            gacc[384:448, 64:128] = gkk[128:192, 192:256]

        def act_g():
            for half in range(2):
                g_p1(half).wait()
            gs[...] = gacc[...] + gr1[...]
            for half in range(2):
                g_p2(half).start()

        def rows_of(k):
            return pl.ds(pl.multiple_of(128 * k, 128), 128)

        def share(slot, k):
            return (remote(tbuf.at[slot, k], tbuf.at[slot, k], d_s.at[slot, 0], d_r.at[slot, 0], dev_sib),
                    remote(gab.at[slot, rows_of(k)], gab.at[slot, rows_of(k)], d_s.at[slot, 1], d_r.at[slot, 1], dev_sib))

        def merge(h, slot):
            for half in range(2):
                g_p2(half).wait()
            g = gs[...] + gr2[...]
            gab[slot, rows_of(core), 0:128] = g[0:128]
            gab[slot, rows_of(core), 128:256] = g[128:256]
            zero = jnp.zeros((64, 64), F32)

            def diag(a, b):
                return jnp.concatenate([jnp.concatenate([a, zero], 1), jnp.concatenate([zero, b], 1)], 0)
            t0, t1, t2, t3 = (tall[i, h] for i in range(4))
            low = g[384:448]
            off = dot(diag(low[:, 0:64], low[:, 64:128]), diag(t1, t3), 1, 0)
            off = -dot(diag(t0, t2), off, 1, 0)
            ta = jnp.concatenate([jnp.concatenate([t0, off[0:64, 0:64]], 1), jnp.concatenate([zero, t1], 1)], 0)
            tb = jnp.concatenate([jnp.concatenate([t2, off[64:128, 64:128]], 1), jnp.concatenate([zero, t3], 1)], 0)
            cross = -dot(ta, dot(g[256:384], tb, 1, 0), 1, 0)
            tbuf[slot, core, 0:128, 0:128] = ta
            tbuf[slot, core, 0:128, 128:256] = cross
            tbuf[slot, core, 128:256, 0:128] = jnp.zeros((128, 128), F32)
            tbuf[slot, core, 128:256, 128:256] = tb
            for cp in share(slot, core):
                cp.start()

        def factor(slot):
            for cp in share(slot, core):
                cp.wait_send()
            for cp in share(slot, 1 - core):
                cp.wait_recv()
            nbuf[...] = dot(tbuf[slot, 0], gab[slot], 1, 0)

        def product(h, slot, p):
            wacc[p] = jnp.zeros((256, 256), F32)
            t0 = rows // TILE - tiles_of(h)

            def one(t, n):
                wacc[p] += dot6([(split(xt[t0 + t + u]), parts(slot, t + u, pl.ds(256 * p, 256)))
                                 for u in range(n)], 1, 0)
            over_tiles(tiles_of(h), one)
            for half in range(2):
                w_p1(p, half).start()

        def act_w(p):
            for half in range(2):
                w_p1(p, half).wait()
            ws[p] = wacc[p] + r1[p]
            for half in range(2):
                w_p2(p, half).start()

        def reduced(p):
            for half in range(2):
                w_p2(p, half).wait()
            return ws[p] + r2[p]

        def update(h, slot, p, y):
            for k, part in enumerate(split(-y)):
                yp[k] = part
            t0 = rows // TILE - tiles_of(h)

            def one(t, n):
                for u in range(n):
                    xt[t0 + t + u] += dot6([(tuple(yp[k] for k in range(3)), parts(slot, t + u, pl.ds(256 * p, 256)))], 1, 1)
            over_tiles(tiles_of(h), one)

        last = blocks - 1
        top = rows // TILE - 1
        issue_v(last)
        v_loc(last).start()
        issue_z(top)
        for hh in range(last - 1, last - AHEAD, -1):
            issue_v(hh)
        v_loc(last - 1).start()
        for t in range(top - 1, top - Z_START, -1):
            issue_z(t)
        forward_v(last)
        collect_v(last)
        prepare(last, last % 2)
        gram(last, last % 2)
        for half in range(2):
            g_p1(half).start()
        forward_v(last - 1)

        def block_step(i, _):
            h = last - i
            slot = h % 2
            nslot = 1 - slot

            @pl.when(slot == 1)
            def _():
                collect_z((h - 1) // 2)

            product(h, slot, 1)
            product(h, slot, 0)

            early = h >= SWITCH
            late = h < SWITCH

            @pl.when(early)
            def _():
                act_g()
                act_w(1)

            @pl.when(late)
            def _():
                merge(h, slot)
            for hh in range(blocks - 2):
                @pl.when(h - 2 == hh)
                def _():
                    forward_v(hh)
            for hh in range(blocks - AHEAD):
                @pl.when(h == hh + AHEAD)
                def _():
                    issue_v(hh)
            for hh in range(blocks - 1):
                @pl.when(h - 1 == hh)
                def _():
                    collect_v(hh)

            @pl.when(h > 0)
            def _():
                prepare(h - 1, nslot)
            for hh in range(blocks - 2):
                @pl.when(h - 2 == hh)
                def _():
                    v_loc(hh).start()

            @pl.when(early)
            def _():
                act_w(0)
                merge(h, slot)

            @pl.when(late)
            def _():
                act_w(1)

            @pl.when(h > 0)
            def _():
                gram(h - 1, nslot)

            @pl.when(late)
            def _():
                act_w(0)

            @pl.when(h > 0)
            def _():
                for half in range(2):
                    g_p1(half).start()

            @pl.when(jnp.logical_and(slot == 1, jnp.logical_and(h >= 3, h <= 2 * (top - Z_START) + 3)))
            def _():
                issue_z((h - 3) // 2)
            factor(slot)
            yb = dot(reduced(1), tbuf[slot, 1], 1, 1)
            wacc[1] = dot(yb, nbuf[...], 1, 1)
            update(h, slot, 1, yb)
            ya = dot(reduced(0), tbuf[slot, 0], 1, 1) - wacc[1]

            update(h, slot, 0, ya)

            @pl.when(jnp.logical_and(h > 0, h <= SWITCH))
            def _():
                act_g()
            return 0

        lax.fori_loop(0, blocks, block_step, 0)
        for t in range(rows // TILE):
            o_ref[TILE * t:TILE * t + TILE, :] = xt[t].T
        for hh in range(blocks):
            v_x(hh).wait_send()
            v_sib(hh).wait_send()
            v_fwd(hh).wait_send()
            for cp in t_copies(hh):
                cp.wait_send()
        for t in range(rows // TILE):
            for cp in z_copies(t):
                cp.wait_send()

    return body


def solution(mesh):
    def local(v_loc, t_loc, z_loc):
        rows, cols = v_loc.shape
        blocks = cols // 128
        t_loc = t_loc.reshape(blocks, 2, 64, 64)
        tiles = ((blocks + 1) // 2) * ((blocks + 2) // 2)
        dma = pltpu.SemaphoreType.DMA
        hbm = pl.BlockSpec(memory_space=pl.ANY)
        return pl.pallas_call(
            make_kernel(rows, blocks),
            out_shape=jax.ShapeDtypeStruct((rows, 256), F32),
            in_specs=[hbm] * 3,
            out_specs=pl.BlockSpec(memory_space=pltpu.VMEM),
            scratch_shapes=[
                pltpu.VMEM((3 * TILE * tiles + 2 * rows, 128), F32),
                pltpu.VMEM((2, 3, rows, 512), BF16),
                pltpu.VMEM((4, blocks, 64, 64), F32),
                pltpu.VMEM((rows // TILE, 256, TILE), F32),
                pltpu.VMEM((2, 256, 256), F32), pltpu.VMEM((2, 256, 256), F32),
                pltpu.VMEM((2, 256, 256), F32), pltpu.VMEM((2, 256, 256), F32),
                pltpu.VMEM((3, 256, 256), BF16),
                pltpu.VMEM((384, 256), F32),
                pltpu.VMEM((448, 128), F32), pltpu.VMEM((448, 128), F32),
                pltpu.VMEM((448, 128), F32), pltpu.VMEM((448, 128), F32),
                pltpu.VMEM((2, 2, 256, 256), F32),
                pltpu.VMEM((2, 256, 256), F32),
                pltpu.VMEM((256, 256), F32),
                dma((blocks,)), dma((blocks,)), dma((blocks,)), dma((blocks,)), dma((3, blocks)),
                dma((blocks,)), dma((blocks,)), dma((blocks,)), dma((blocks,)), dma((4, blocks)),
                dma((3, rows // TILE)), dma((rows // TILE,)), dma((4, rows // TILE)),
                dma((2, 2)), dma((2, 2)), dma((2, 2)), dma((2, 2)),
                dma((2,)), dma((2,)), dma((2,)), dma((2,)),
                dma((2, 2)), dma((2, 2)),
            ],
            compiler_params=pltpu.CompilerParams(collective_id=0, has_side_effects=True,
                                                 vmem_limit_bytes=67043328),
        )(v_loc, t_loc, z_loc.T)

    return jax.shard_map(local, mesh=mesh,
                         in_specs=(P('row', 'col'), P('col', None, None), P(None, ('col', 'row'))),
                         out_specs=P('row', 'col'), check_vma=False)
```

time: 336 us -> 316 us (0.940)
  Pallas kernels: 333 us -> 313 us
    pallas_call x1, Pallas kernels: 333 us -> 313 us  [local(): pl.pallas_call(make_kernel(rows, blocks), out_shape=jax.ShapeDtypeStruct(...]
where the time goes in v3:
time: 316 us
  Pallas kernels  313 us (99%)
    pallas_call x1, Pallas kernels, local(): pl.pallas_call(make_kernel(rows, blocks), out_shape=jax.ShapeDtypeStruct(...  313 us

profile of v3, /device:TPU:0, one launch (start us, length us, event | category | flops | bytes accessed | tf_op | source)
XLA Modules:
  0.0 316.3 jit_solution(7834067519384768250)
XLA Ops:
  0.0 313.2 %shard_map.37 = f32[2048,256]{1,0:T(8,128)} custom-call(f32[2048,2048]{1,0:T(8,128)} %v_hbm.1, f32[16,2,64,64]{3,2,1,0:T(8,128)} %bitcast.3, f32[64,8192]{1,0:T(8,128)} %bitcast.2), custom_call_target="tpu_custom_call" | custom-call | tf_op jit(solution)/shard_map/pallas_call | solution.py:420
  313.2 3.0 copy.5

commit v4 on v3

--- a/solution.py
+++ b/solution.py
@@ -10,8 +10,7 @@
 MESH = pl.DeviceIdType.MESH
 TILE = 256
 AHEAD = 8
-Z_START = 4
-SWITCH = 10
+Z_START = 3
 
 
 def dot(a, b, ca, cb):
@@ -45,9 +44,9 @@
 
     area = TILE * tiles_before(-1)
 
-    def body(v_hbm, t_hbm, z_hbm, o_ref, vbuf, vp, tall, xt, wacc, r1, ws, r2, yp, gkk, gacc, gr1, gs, gr2, tbuf, gab,
+    def body(v_hbm, t_hbm, z_hbm, o_hbm, vbuf, vp, tall, xt, wacc, r1, ws, r2, yp, gkk, gacc, gr1, gr2, gf, tbuf, gab,
              nbuf, vx_s, vsib_s, vfwd_s, vloc_s, v_r, tx_s, txc_s, tsib_s, tloc_s, t_r, z_s, zloc_s, z_r,
-             p1_s, p1_r, p2_s, p2_r, g1_s, g1_r, g2_s, g2_r, d_s, d_r):
+             p1_s, p1_r, p2_s, p2_r, g_s, g_r, d_s, d_r, o_s):
         r = lax.axis_index("row")
         c = lax.axis_index("col")
         core = c % 2
@@ -65,11 +64,14 @@
         pl.semaphore_wait(barrier, 6)
 
         def v_src(hh):
-            n = TILE * tiles_of(hh)
+            n = 128 * (blocks - hh)
             return v_hbm.at[pl.ds(rows - n, n), pl.ds(hh * 128, 128)]
 
+        def v_rows(base, hh):
+            return vbuf.at[pl.ds(base + 128 * (hh % 2), 128 * (blocks - hh)), :]
+
         def v_dst(rel, hh):
-            return vbuf.at[pl.ds(area * (rel - 1) + TILE * tiles_before(hh), TILE * tiles_of(hh)), :]
+            return v_rows(area * (rel - 1) + TILE * tiles_before(hh), hh)
 
         def v_x(hh):
             return remote(v_src(hh), v_dst(2, hh), vx_s.at[hh], v_r.at[1, hh], dev_x)
@@ -81,8 +83,13 @@
             return remote(v_dst(2, hh), v_dst(3, hh), vfwd_s.at[hh], v_r.at[2, hh], dev_sib)
 
         def v_loc(hh):
-            dst = vbuf.at[pl.ds(3 * area + rows * (hh % 2), TILE * tiles_of(hh)), :]
-            return pltpu.make_async_copy(v_src(hh), dst, vloc_s.at[hh])
+            return pltpu.make_async_copy(v_src(hh), v_rows(3 * area + rows * (hh % 2), hh), vloc_s.at[hh])
+
+        def clear_v():
+            for rel in range(3):
+                for hh in range(1, blocks, 2):
+                    vbuf[pl.ds(area * rel + TILE * tiles_before(hh), 128), :] = jnp.zeros((128, 128), F32)
+            vbuf[pl.ds(3 * area + rows, 128), :] = jnp.zeros((128, 128), F32)
 
         def v_arrive(rel, hh):
             return remote(v_src(hh), v_dst(rel, hh), vx_s.at[hh], v_r.at[rel - 1, hh], dev_x)
@@ -151,13 +158,53 @@
             s = pl.ds(128 * half, 128)
             return remote(ws.at[p, s], r2.at[p, s], p2_s.at[p, half], p2_r.at[p, half], steps(half)[1])
 
-        def g_p1(half):
-            s = pl.ds(224 * half, 224)
-            return remote(gacc.at[s], gr1.at[s], g1_s.at[half], g1_r.at[half], steps(half)[0])
-
-        def g_p2(half):
-            s = pl.ds(224 * half, 224)
-            return remote(gs.at[s], gr2.at[s], g2_s.at[half], g2_r.at[half], steps(half)[1])
+        def g_place(f):
+            k1, k2 = ((r % 2), (r // 2)) if f == 0 else ((r // 2), (r % 2))
+            return 224 * f, k1, k2
+
+        def g_rows(start, n):
+            return pl.ds(pl.multiple_of(start, 8), n)
+
+        def g_rs1(par, f):
+            base, k1, _ = g_place(f)
+            s = g_rows(base + 112 * (1 - k1), 112)
+            return remote(gacc.at[par, s], gr1.at[par, s], g_s.at[0, par, f], g_r.at[0, par, f], steps(f)[0])
+
+        def g_rs2(par, f):
+            base, k1, k2 = g_place(f)
+            s = g_rows(base + 112 * k1 + 56 * (1 - k2), 56)
+            return remote(gacc.at[par, s], gr2.at[par, s], g_s.at[1, par, f], g_r.at[1, par, f], steps(f)[1])
+
+        def g_ag2(par, f):
+            base, k1, k2 = g_place(f)
+            s = g_rows(base + 112 * k1 + 56 * k2, 56)
+            return remote(gf.at[par, s], gf.at[par, s], g_s.at[2, par, f], g_r.at[2, par, f], steps(f)[1])
+
+        def g_ag1(par, f):
+            base, k1, _ = g_place(f)
+            s = g_rows(base + 112 * k1, 112)
+            return remote(gf.at[par, s], gf.at[par, s], g_s.at[3, par, f], g_r.at[3, par, f], steps(f)[0])
+
+        def act_rs2(par):
+            for f in range(2):
+                base, k1, _ = g_place(f)
+                g_rs1(par, f).wait()
+                s = g_rows(base + 112 * k1, 112)
+                gacc[par, s] = gacc[par, s] + gr1[par, s]
+                g_rs2(par, f).start()
+
+        def act_ag2(par):
+            for f in range(2):
+                base, k1, k2 = g_place(f)
+                g_rs2(par, f).wait()
+                s = g_rows(base + 112 * k1 + 56 * k2, 56)
+                gf[par, s] = gacc[par, s] + gr2[par, s]
+                g_ag2(par, f).start()
+
+        def act_ag1(par):
+            for f in range(2):
+                g_ag2(par, f).wait()
+                g_ag1(par, f).start()
 
         def over_tiles(n, fn):
             def four(t, _):
@@ -172,6 +219,12 @@
             @pl.when(n % 2 == 1)
             def _():
                 fn(n - 1, 1)
+
+        def whole(n, fn):
+            for k in range(1, rows // TILE + 1):
+                @pl.when(n == k)
+                def _():
+                    fn(0, k)
 
         def prepare(h, slot):
             bases = []
@@ -209,18 +262,15 @@
                 gkk[256:384, :] += dot6([(parts(slot, t + u, half), parts(slot, t + u, pl.ds(256, 256)))
                                          for u in range(n)], 0, 0)
             over_tiles(tiles_of(h), one)
-            gacc[0:128, :] = gkk[256:384, 0:128]
-            gacc[128:256, :] = gkk[256:384, 128:256]
-            gacc[256:384, :] = gkk[0:128, 128:256]
-            gacc[384:448, 0:64] = gkk[0:64, 64:128]
-            gacc[384:448, 64:128] = gkk[128:192, 192:256]
-
-        def act_g():
-            for half in range(2):
-                g_p1(half).wait()
-            gs[...] = gacc[...] + gr1[...]
-            for half in range(2):
-                g_p2(half).start()
+
+        def send_g(par):
+            gacc[par, 0:128, :] = gkk[256:384, 0:128]
+            gacc[par, 128:256, :] = gkk[256:384, 128:256]
+            gacc[par, 256:384, :] = gkk[0:128, 128:256]
+            gacc[par, 384:448, 0:64] = gkk[0:64, 64:128]
+            gacc[par, 384:448, 64:128] = gkk[128:192, 192:256]
+            for f in range(2):
+                g_rs1(par, f).start()
 
         def rows_of(k):
             return pl.ds(pl.multiple_of(128 * k, 128), 128)
@@ -230,9 +280,9 @@
                     remote(gab.at[slot, rows_of(k)], gab.at[slot, rows_of(k)], d_s.at[slot, 1], d_r.at[slot, 1], dev_sib))
 
         def merge(h, slot):
-            for half in range(2):
-                g_p2(half).wait()
-            g = gs[...] + gr2[...]
+            for f in range(2):
+                g_ag1(slot, f).wait()
+            g = gf[slot]
             gab[slot, rows_of(core), 0:128] = g[0:128]
             gab[slot, rows_of(core), 128:256] = g[128:256]
             zero = jnp.zeros((64, 64), F32)
@@ -258,16 +308,21 @@
                 cp.wait_send()
             for cp in share(slot, 1 - core):
                 cp.wait_recv()
-            nbuf[...] = dot(tbuf[slot, 0], gab[slot], 1, 0)
-
-        def product(h, slot, p):
+            tb = tbuf[slot, 1]
+            nbuf[0:256, :] = tb
+            nbuf[256:512, :] = dot(dot(tbuf[slot, 0], gab[slot], 1, 0), tb, 1, 0)
+
+        def product(h, slot, p, only=0):
             wacc[p] = jnp.zeros((256, 256), F32)
             t0 = rows // TILE - tiles_of(h)
 
             def one(t, n):
                 wacc[p] += dot6([(split(xt[t0 + t + u]), parts(slot, t + u, pl.ds(256 * p, 256)))
                                  for u in range(n)], 1, 0)
-            over_tiles(tiles_of(h), one)
+            if only:
+                one(0, only)
+            else:
+                whole(tiles_of(h), one)
             for half in range(2):
                 w_p1(p, half).start()
 
@@ -291,7 +346,12 @@
             def one(t, n):
                 for u in range(n):
                     xt[t0 + t + u] += dot6([(tuple(yp[k] for k in range(3)), parts(slot, t + u, pl.ds(256 * p, 256)))], 1, 1)
-            over_tiles(tiles_of(h), one)
+            whole(tiles_of(h), one)
+
+        def ready(h, slot):
+            collect_v(h)
+            prepare(h, slot)
+            gram(h, slot)
 
         last = blocks - 1
         top = rows // TILE - 1
@@ -303,99 +363,109 @@
         v_loc(last - 1).start()
         for t in range(top - 1, top - Z_START, -1):
             issue_z(t)
+        clear_v()
         forward_v(last)
-        collect_v(last)
-        prepare(last, last % 2)
-        gram(last, last % 2)
-        for half in range(2):
-            g_p1(half).start()
+        ready(last, last % 3)
+        send_g(last % 2)
+        collect_z(top)
+        for p in (1, 0):
+            product(last, last % 3, p, only=1)
         forward_v(last - 1)
+        v_loc(last - 2).start()
+        ready(last - 1, (last - 1) % 3)
+        act_rs2(last % 2)
+        send_g((last - 1) % 2)
+        act_w(1)
+        act_ag2(last % 2)
+        act_w(0)
+        act_ag1(last % 2)
+        act_rs2((last - 1) % 2)
+        forward_v(last - 2)
 
         def block_step(i, _):
             h = last - i
             slot = h % 2
-            nslot = 1 - slot
-
-            @pl.when(slot == 1)
+            vslot = h % 3
+
+            @pl.when(jnp.logical_and(slot == 1, h < last))
             def _():
                 collect_z((h - 1) // 2)
 
-            product(h, slot, 1)
-            product(h, slot, 0)
-
-            early = h >= SWITCH
-            late = h < SWITCH
-
-            @pl.when(early)
-            def _():
-                act_g()
-                act_w(1)
-
-            @pl.when(late)
-            def _():
-                merge(h, slot)
-            for hh in range(blocks - 2):
-                @pl.when(h - 2 == hh)
+            @pl.when(h < last)
+            def _():
+                product(h, vslot, 1)
+                product(h, vslot, 0)
+            merge(h, slot)
+
+            @pl.when(jnp.logical_and(h > 0, h < last))
+            def _():
+                act_rs2(1 - slot)
+            for hh in range(blocks - 3):
+                @pl.when(h - 3 == hh)
                 def _():
                     forward_v(hh)
             for hh in range(blocks - AHEAD):
                 @pl.when(h == hh + AHEAD)
                 def _():
                     issue_v(hh)
-            for hh in range(blocks - 1):
-                @pl.when(h - 1 == hh)
-                def _():
-                    collect_v(hh)
-
-            @pl.when(h > 0)
-            def _():
-                prepare(h - 1, nslot)
             for hh in range(blocks - 2):
                 @pl.when(h - 2 == hh)
                 def _():
+                    collect_v(hh)
+
+            @pl.when(h > 1)
+            def _():
+                prepare(h - 2, (h - 2) % 3)
+            for hh in range(blocks - 3):
+                @pl.when(h - 3 == hh)
+                def _():
                     v_loc(hh).start()
-
-            @pl.when(early)
+            @pl.when(h < last)
+            def _():
+                act_w(1)
+
+            @pl.when(h > 1)
+            def _():
+                gram(h - 2, (h - 2) % 3)
+
+            @pl.when(h < last)
             def _():
                 act_w(0)
-                merge(h, slot)
-
-            @pl.when(late)
-            def _():
-                act_w(1)
 
             @pl.when(h > 0)
             def _():
-                gram(h - 1, nslot)
-
-            @pl.when(late)
-            def _():
-                act_w(0)
-
-            @pl.when(h > 0)
-            def _():
-                for half in range(2):
-                    g_p1(half).start()
+                act_ag2(1 - slot)
+
+            @pl.when(h > 1)
+            def _():
+                send_g(slot)
 
             @pl.when(jnp.logical_and(slot == 1, jnp.logical_and(h >= 3, h <= 2 * (top - Z_START) + 3)))
             def _():
                 issue_z((h - 3) // 2)
             factor(slot)
-            yb = dot(reduced(1), tbuf[slot, 1], 1, 1)
-            wacc[1] = dot(yb, nbuf[...], 1, 1)
-            update(h, slot, 1, yb)
+            yb = dot(reduced(1), nbuf[...], 1, 1)
+            wacc[1] = yb[:, 256:512]
+            update(h, vslot, 1, yb[:, 0:256])
             ya = dot(reduced(0), tbuf[slot, 0], 1, 1) - wacc[1]
-
-            update(h, slot, 0, ya)
-
-            @pl.when(jnp.logical_and(h > 0, h <= SWITCH))
-            def _():
-                act_g()
+            update(h, vslot, 0, ya)
+
+            @pl.when(h > 0)
+            def _():
+                act_ag1(1 - slot)
             return 0
 
         lax.fori_loop(0, blocks, block_step, 0)
+        stages = [buf.at[k] for buf in (wacc, r1, ws, r2) for k in range(2)]
+        outs = []
         for t in range(rows // TILE):
-            o_ref[TILE * t:TILE * t + TILE, :] = xt[t].T
+            if t >= len(stages):
+                outs[t - len(stages)].wait()
+            stages[t % len(stages)][...] = xt[t].T
+            outs.append(pltpu.make_async_copy(stages[t % len(stages)], o_hbm.at[pl.ds(TILE * t, TILE), :], o_s.at[t]))
+            outs[t].start()
+        for cp in outs[-len(stages):]:
+            cp.wait()
         for hh in range(blocks):
             v_x(hh).wait_send()
             v_sib(hh).wait_send()
@@ -421,27 +491,27 @@
             make_kernel(rows, blocks),
             out_shape=jax.ShapeDtypeStruct((rows, 256), F32),
             in_specs=[hbm] * 3,
-            out_specs=pl.BlockSpec(memory_space=pltpu.VMEM),
+            out_specs=hbm,
             scratch_shapes=[
                 pltpu.VMEM((3 * TILE * tiles + 2 * rows, 128), F32),
-                pltpu.VMEM((2, 3, rows, 512), BF16),
+                pltpu.VMEM((3, 3, rows, 512), BF16),
                 pltpu.VMEM((4, blocks, 64, 64), F32),
                 pltpu.VMEM((rows // TILE, 256, TILE), F32),
                 pltpu.VMEM((2, 256, 256), F32), pltpu.VMEM((2, 256, 256), F32),
                 pltpu.VMEM((2, 256, 256), F32), pltpu.VMEM((2, 256, 256), F32),
                 pltpu.VMEM((3, 256, 256), BF16),
                 pltpu.VMEM((384, 256), F32),
-                pltpu.VMEM((448, 128), F32), pltpu.VMEM((448, 128), F32),
-                pltpu.VMEM((448, 128), F32), pltpu.VMEM((448, 128), F32),
+                pltpu.VMEM((2, 448, 128), F32), pltpu.VMEM((2, 448, 128), F32),
+                pltpu.VMEM((2, 448, 128), F32), pltpu.VMEM((2, 448, 128), F32),
                 pltpu.VMEM((2, 2, 256, 256), F32),
                 pltpu.VMEM((2, 256, 256), F32),
-                pltpu.VMEM((256, 256), F32),
+                pltpu.VMEM((512, 256), F32),
                 dma((blocks,)), dma((blocks,)), dma((blocks,)), dma((blocks,)), dma((3, blocks)),
                 dma((blocks,)), dma((blocks,)), dma((blocks,)), dma((blocks,)), dma((4, blocks)),
                 dma((3, rows // TILE)), dma((rows // TILE,)), dma((4, rows // TILE)),
                 dma((2, 2)), dma((2, 2)), dma((2, 2)), dma((2, 2)),
-                dma((2,)), dma((2,)), dma((2,)), dma((2,)),
-                dma((2, 2)), dma((2, 2)),
+                dma((4, 2, 2)), dma((4, 2, 2)),
+                dma((2, 2)), dma((2, 2)), dma((rows // TILE,)),
             ],
             compiler_params=pltpu.CompilerParams(collective_id=0, has_side_effects=True,
                                                  vmem_limit_bytes=67043328),

time: 316 us -> 294 us (0.930)
  Pallas kernels: 313 us -> 290 us
    pallas_call x1, Pallas kernels: 313 us -> 290 us  [local(): pl.pallas_call(make_kernel(rows, blocks), out_shape=jax.ShapeDtypeStruct(...]
where the time goes in v4:
time: 294 us
  Pallas kernels  290 us (99%)
  local copies, waits for them, and re-layouts  3.05 us (1%)
    pallas_call x1, Pallas kernels, local(): pl.pallas_call(make_kernel(rows, blocks), out_shape=jax.ShapeDtypeStruct(...  290 us

profile of v4, /device:TPU:0, one launch (start us, length us, event | category | flops | bytes accessed | tf_op | source)
XLA Modules:
  0.0 293.5 jit_solution(14226664177362607798)
XLA Ops:
  0.0 290.5 %shard_map.37 = f32[2048,256]{1,0:T(8,128)} custom-call(f32[2048,2048]{1,0:T(8,128)} %v_hbm.1, f32[16,2,64,64]{3,2,1,0:T(8,128)} %bitcast.3, f32[64,8192]{1,0:T(8,128)} %bitcast.2), custom_call_target="tpu_custom_call" | custom-call | tf_op jit(solution)/shard_map/pallas_call | solution.py:490
  290.5 3.0 %copy.5 = f32[2048,256]{1,0:T(8,128)} copy(f32[2048,256]{1,0:T(8,128)} %shard_map.37) | data formatting | bytes 4194304

commit v5 on v4

--- a/solution.py
+++ b/solution.py
@@ -10,7 +10,7 @@
 MESH = pl.DeviceIdType.MESH
 TILE = 256
 AHEAD = 8
-Z_START = 3
+GATHER = 8
 
 
 def dot(a, b, ca, cb):
@@ -46,7 +46,7 @@
 
     def body(v_hbm, t_hbm, z_hbm, o_hbm, vbuf, vp, tall, xt, wacc, r1, ws, r2, yp, gkk, gacc, gr1, gr2, gf, tbuf, gab,
              nbuf, vx_s, vsib_s, vfwd_s, vloc_s, v_r, tx_s, txc_s, tsib_s, tloc_s, t_r, z_s, zloc_s, z_r,
-             p1_s, p1_r, p2_s, p2_r, g_s, g_r, d_s, d_r, o_s):
+             p1_s, p1_r, p2_s, p2_r, g_s, g_r, w_s, w_r, d_s, d_r, o_s):
         r = lax.axis_index("row")
         c = lax.axis_index("col")
         core = c % 2
@@ -55,6 +55,8 @@
         dev_x, dev_sib, dev_xc = (r, cx), (r, csib), (r, cxc)
         dev_y, dev_z, dev_d = (ry, c), (rz, c), (rd, c)
 
+        last = blocks - 1
+
         def remote(src, dst, ss, rs, dev):
             return pltpu.make_async_remote_copy(src, dst, ss, rs, device_id=dev, device_id_type=MESH)
 
@@ -106,11 +108,11 @@
             return remote(t_hbm.at[h, core], tall.at[slot, h], tx_s.at[h], t_r.at[slot, h], dev_x)
 
         def issue_v(hh):
+            v_x(hh).start()
+            v_sib(hh).start()
             for cp in t_copies(hh):
                 cp.start()
             t_loc(hh).start()
-            v_x(hh).start()
-            v_sib(hh).start()
 
         def forward_v(hh):
             v_arrive(2, hh).wait_recv()
@@ -124,28 +126,30 @@
             for slot in (cx, csib, cxc):
                 t_arrive(slot, hh).wait_recv()
 
-        def z_src(to, t):
-            return z_hbm.at[:, pl.ds(pl.multiple_of(rows * to + TILE * t, TILE), TILE)]
-
-        def z_dst(src_r, t):
-            return xt.at[t, pl.ds(pl.multiple_of(64 * src_r, 64), 64), :]
-
-        def z_copies(t):
-            return [remote(z_src(dev[0], t), z_dst(r, t), z_s.at[i, t], z_r.at[r, t], dev)
+        def z_src(to, t, part):
+            return z_hbm.at[:, pl.ds(pl.multiple_of(rows * to + TILE * t + 128 * part, 128), 128)]
+
+        def z_dst(src_r, t, part):
+            return xt.at[t, pl.ds(pl.multiple_of(64 * src_r, 64), 64), pl.ds(128 * part, 128)]
+
+        def z_copies(t, part):
+            return [remote(z_src(dev[0], t, part), z_dst(r, t, part), z_s.at[i, t, part], z_r.at[r, t, part], dev)
                     for i, dev in enumerate((dev_y, dev_z, dev_d))]
 
-        def z_loc(t):
-            return pltpu.make_async_copy(z_src(r, t), z_dst(r, t), zloc_s.at[t])
-
-        def issue_z(t):
-            for cp in z_copies(t):
+        def z_loc(t, part):
+            return pltpu.make_async_copy(z_src(r, t, part), z_dst(r, t, part), zloc_s.at[t, part])
+
+        def issue_z(t, part):
+            for cp in z_copies(t, part):
                 cp.start()
-            z_loc(t).start()
+            z_loc(t, part).start()
 
         def collect_z(t):
-            z_loc(t).wait()
-            for src_r in (ry, rz, rd):
-                remote(z_src(r, t), z_dst(src_r, t), z_s.at[0, t], z_r.at[src_r, t], dev_y).wait_recv()
+            for part in range(2):
+                z_loc(t, part).wait()
+                for src_r in (ry, rz, rd):
+                    dst = z_dst(src_r, t, part)
+                    remote(z_src(r, t, part), dst, z_s.at[0, t, part], z_r.at[src_r, t, part], dev_y).wait_recv()
 
         def steps(half):
             return (dev_y, dev_z) if half == 0 else (dev_z, dev_y)
@@ -164,6 +168,53 @@
 
         def g_rows(start, n):
             return pl.ds(pl.multiple_of(start, 8), n)
+
+        def w_kept(f, other=0):
+            k1 = r % 2 if f == 0 else r // 2
+            return g_rows(128 * f + 64 * (k1 + other * (1 - 2 * k1)), 64)
+
+        def w_e1(p, f):
+            s = w_kept(f, 1)
+            return remote(wacc.at[p, s], r1.at[p, s], w_s.at[0, p, f], w_r.at[0, p, f], steps(f)[0])
+
+        def w_e2(p, f):
+            s = w_kept(f)
+            return remote(ws.at[p, s], r2.at[p, s], w_s.at[1, p, f], w_r.at[1, p, f], steps(f)[1])
+
+        def w_e3(p, f):
+            s = w_kept(f)
+            return remote(wacc.at[p, s], wacc.at[p, s], w_s.at[2, p, f], w_r.at[2, p, f], steps(f)[0])
+
+        def w_act1(p):
+            for f in range(2):
+                w_e1(p, f).wait()
+            for f in range(2):
+                s = w_kept(f)
+                ws[p, s] = wacc[p, s] + r1[p, s]
+                w_e2(p, f).start()
+
+        def w_act2(p):
+            for f in range(2):
+                w_e2(p, f).wait()
+            for f in range(2):
+                s = w_kept(f)
+                wacc[p, s] = ws[p, s] + r2[p, s]
+                w_e3(p, f).start()
+
+        def g_p1(par, f):
+            s = pl.ds(224 * f, 224)
+            return remote(gacc.at[par, s], gr1.at[par, s], g_s.at[0, par, f], g_r.at[0, par, f], steps(f)[0])
+
+        def g_p2(par, f):
+            s = pl.ds(224 * f, 224)
+            return remote(gacc.at[par, s], gr2.at[par, s], g_s.at[1, par, f], g_r.at[1, par, f], steps(f)[1])
+
+        def act_p2(par):
+            for f in range(2):
+                g_p1(par, f).wait()
+            gacc[par] = gacc[par] + gr1[par]
+            for f in range(2):
+                g_p2(par, f).start()
 
         def g_rs1(par, f):
             base, k1, _ = g_place(f)
@@ -187,8 +238,9 @@
 
         def act_rs2(par):
             for f in range(2):
+                g_rs1(par, f).wait()
+            for f in range(2):
                 base, k1, _ = g_place(f)
-                g_rs1(par, f).wait()
                 s = g_rows(base + 112 * k1, 112)
                 gacc[par, s] = gacc[par, s] + gr1[par, s]
                 g_rs2(par, f).start()
@@ -263,14 +315,14 @@
                                          for u in range(n)], 0, 0)
             over_tiles(tiles_of(h), one)
 
-        def send_g(par):
+        def send_g(par, first=g_rs1):
             gacc[par, 0:128, :] = gkk[256:384, 0:128]
             gacc[par, 128:256, :] = gkk[256:384, 128:256]
             gacc[par, 256:384, :] = gkk[0:128, 128:256]
             gacc[par, 384:448, 0:64] = gkk[0:64, 64:128]
             gacc[par, 384:448, 64:128] = gkk[128:192, 192:256]
             for f in range(2):
-                g_rs1(par, f).start()
+                first(par, f).start()
 
         def rows_of(k):
             return pl.ds(pl.multiple_of(128 * k, 128), 128)
@@ -280,8 +332,16 @@
                     remote(gab.at[slot, rows_of(k)], gab.at[slot, rows_of(k)], d_s.at[slot, 1], d_r.at[slot, 1], dev_sib))
 
         def merge(h, slot):
-            for f in range(2):
-                g_ag1(slot, f).wait()
+            @pl.when(h >= last - 1)
+            def _():
+                for f in range(2):
+                    g_p2(slot, f).wait()
+                gf[slot] = gacc[slot] + gr2[slot]
+
+            @pl.when(h < last - 1)
+            def _():
+                for f in range(2):
+                    g_ag1(slot, f).wait()
             g = gf[slot]
             gab[slot, rows_of(core), 0:128] = g[0:128]
             gab[slot, rows_of(core), 128:256] = g[128:256]
@@ -312,19 +372,38 @@
             nbuf[0:256, :] = tb
             nbuf[256:512, :] = dot(dot(tbuf[slot, 0], gab[slot], 1, 0), tb, 1, 0)
 
-        def product(h, slot, p, only=0):
-            wacc[p] = jnp.zeros((256, 256), F32)
+        def gathered(h):
+            return jnp.logical_and(h >= GATHER, h < last)
+
+        def pairwise(h):
+            return jnp.logical_or(h < GATHER, h == last)
+
+        def product(h, slot, run):
             t0 = rows // TILE - tiles_of(h)
 
-            def one(t, n):
-                wacc[p] += dot6([(split(xt[t0 + t + u]), parts(slot, t + u, pl.ds(256 * p, 256)))
-                                 for u in range(n)], 1, 0)
-            if only:
-                one(0, only)
-            else:
-                whole(tiles_of(h), one)
-            for half in range(2):
-                w_p1(p, half).start()
+            def group(i, _):
+                p = 1 - i
+                wacc[p] = jnp.zeros((256, 256), F32)
+                lanes = pl.ds(pl.multiple_of(256 * p, 256), 256)
+
+                def one(t, n):
+                    wacc[p] += dot6([(split(xt[t0 + t + u]), parts(slot, t + u, lanes)) for u in range(n)], 1, 0)
+                run(tiles_of(h), one)
+                if run is whole:
+                    @pl.when(gathered(h))
+                    def _():
+                        for f in range(2):
+                            w_e1(p, f).start()
+
+                    @pl.when(h < GATHER)
+                    def _():
+                        for half in range(2):
+                            w_p1(p, half).start()
+                else:
+                    for half in range(2):
+                        w_p1(p, half).start()
+                return 0
+            lax.fori_loop(0, 2, group, 0)
 
         def act_w(p):
             for half in range(2):
@@ -333,10 +412,18 @@
             for half in range(2):
                 w_p2(p, half).start()
 
-        def reduced(p):
-            for half in range(2):
-                w_p2(p, half).wait()
-            return ws[p] + r2[p]
+        def reduced(h, p):
+            @pl.when(gathered(h))
+            def _():
+                for f in range(2):
+                    w_e3(p, f).wait()
+
+            @pl.when(pairwise(h))
+            def _():
+                for half in range(2):
+                    w_p2(p, half).wait()
+                wacc[p] = ws[p] + r2[p]
+            return wacc[p]
 
         def update(h, slot, p, y):
             for k, part in enumerate(split(-y)):
@@ -353,33 +440,34 @@
             prepare(h, slot)
             gram(h, slot)
 
-        last = blocks - 1
+        def ready(h, slot):
+            collect_v(h)
+            prepare(h, slot)
+            gram(h, slot)
+
         top = rows // TILE - 1
         issue_v(last)
         v_loc(last).start()
-        issue_z(top)
+        for part in range(2):
+            issue_z(top, part)
         for hh in range(last - 1, last - AHEAD, -1):
             issue_v(hh)
         v_loc(last - 1).start()
-        for t in range(top - 1, top - Z_START, -1):
-            issue_z(t)
+        for part in range(2):
+            issue_z(top - 1, part)
         clear_v()
         forward_v(last)
         ready(last, last % 3)
-        send_g(last % 2)
+        send_g(last % 2, g_p1)
         collect_z(top)
-        for p in (1, 0):
-            product(last, last % 3, p, only=1)
+        product(last, last % 3, lambda n, fn: fn(0, 1))
         forward_v(last - 1)
         v_loc(last - 2).start()
         ready(last - 1, (last - 1) % 3)
-        act_rs2(last % 2)
-        send_g((last - 1) % 2)
+        act_p2(last % 2)
         act_w(1)
-        act_ag2(last % 2)
         act_w(0)
-        act_ag1(last % 2)
-        act_rs2((last - 1) % 2)
+        send_g((last - 1) % 2, g_p1)
         forward_v(last - 2)
 
         def block_step(i, _):
@@ -393,17 +481,24 @@
 
             @pl.when(h < last)
             def _():
-                product(h, vslot, 1)
-                product(h, vslot, 0)
-            merge(h, slot)
+                product(h, vslot, whole)
+
+            @pl.when(gathered(h))
+            def _():
+                w_act1(1)
+                w_act1(0)
+
+            @pl.when(h != last - 1)
+            def _():
+                merge(h, slot)
+
+            @pl.when(h == last - 1)
+            def _():
+                act_p2(slot)
 
             @pl.when(jnp.logical_and(h > 0, h < last))
             def _():
                 act_rs2(1 - slot)
-            for hh in range(blocks - 3):
-                @pl.when(h - 3 == hh)
-                def _():
-                    forward_v(hh)
             for hh in range(blocks - AHEAD):
                 @pl.when(h == hh + AHEAD)
                 def _():
@@ -420,19 +515,29 @@
                 @pl.when(h - 3 == hh)
                 def _():
                     v_loc(hh).start()
-            @pl.when(h < last)
+
+            @pl.when(h < GATHER)
             def _():
                 act_w(1)
 
+            @pl.when(gathered(h))
+            def _():
+                w_act2(1)
+                w_act2(0)
+
             @pl.when(h > 1)
             def _():
                 gram(h - 2, (h - 2) % 3)
 
-            @pl.when(h < last)
+            @pl.when(h < GATHER)
             def _():
                 act_w(0)
 
-            @pl.when(h > 0)
+            @pl.when(h == last - 1)
+            def _():
+                merge(h, slot)
+
+            @pl.when(jnp.logical_and(h > 0, h < last))
             def _():
                 act_ag2(1 - slot)
 
@@ -440,17 +545,27 @@
             def _():
                 send_g(slot)
 
-            @pl.when(jnp.logical_and(slot == 1, jnp.logical_and(h >= 3, h <= 2 * (top - Z_START) + 3)))
-            def _():
-                issue_z((h - 3) // 2)
+            @pl.when(h == last)
+            def _():
+                for part in range(2):
+                    issue_z(top - 2, part)
+
+            @pl.when(jnp.logical_and(h <= last - 2, h >= last - top + 1))
+            def _():
+                for part in range(2):
+                    issue_z(h - (last - top + 1), part)
+            for hh in range(blocks - 3):
+                @pl.when(h - 3 == hh)
+                def _():
+                    forward_v(hh)
             factor(slot)
-            yb = dot(reduced(1), nbuf[...], 1, 1)
-            wacc[1] = yb[:, 256:512]
+            yb = dot(reduced(h, 1), nbuf[...], 1, 1)
+            ws[1] = yb[:, 256:512]
             update(h, vslot, 1, yb[:, 0:256])
-            ya = dot(reduced(0), tbuf[slot, 0], 1, 1) - wacc[1]
+            ya = dot(reduced(h, 0), tbuf[slot, 0], 1, 1) - ws[1]
             update(h, vslot, 0, ya)
 
-            @pl.when(h > 0)
+            @pl.when(jnp.logical_and(h > 0, h < last))
             def _():
                 act_ag1(1 - slot)
             return 0
@@ -473,8 +588,9 @@
             for cp in t_copies(hh):
                 cp.wait_send()
         for t in range(rows // TILE):
-            for cp in z_copies(t):
-                cp.wait_send()
+            for part in range(2):
+                for cp in z_copies(t, part):
+                    cp.wait_send()
 
     return body
 
@@ -508,9 +624,9 @@
                 pltpu.VMEM((512, 256), F32),
                 dma((blocks,)), dma((blocks,)), dma((blocks,)), dma((blocks,)), dma((3, blocks)),
                 dma((blocks,)), dma((blocks,)), dma((blocks,)), dma((blocks,)), dma((4, blocks)),
-                dma((3, rows // TILE)), dma((rows // TILE,)), dma((4, rows // TILE)),
+                dma((3, rows // TILE, 2)), dma((rows // TILE, 2)), dma((4, rows // TILE, 2)),
                 dma((2, 2)), dma((2, 2)), dma((2, 2)), dma((2, 2)),
-                dma((4, 2, 2)), dma((4, 2, 2)),
+                dma((4, 2, 2)), dma((4, 2, 2)), dma((4, 2, 2)), dma((4, 2, 2)),
                 dma((2, 2)), dma((2, 2)), dma((rows // TILE,)),
             ],
             compiler_params=pltpu.CompilerParams(collective_id=0, has_side_effects=True,

time: 294 us -> 286 us (0.973)
  Pallas kernels: 290 us -> 283 us
    pallas_call x1, Pallas kernels: 290 us -> 283 us  [local(): pl.pallas_call(make_kernel(rows, blocks), out_shape=jax.ShapeDtypeStruct(...]
where the time goes in v5:
time: 286 us
  Pallas kernels  283 us (99%)
  local copies, waits for them, and re-layouts  3.05 us (1%)
    pallas_call x1, Pallas kernels, local(): pl.pallas_call(make_kernel(rows, blocks), out_shape=jax.ShapeDtypeStruct(...  283 us

profile of v5, /device:TPU:0, one launch (start us, length us, event | category | flops | bytes accessed | tf_op | source)
XLA Modules:
  0.0 285.8 jit_solution(4726177016300770928)
XLA Ops:
  0.0 282.7 %shard_map.37 = f32[2048,256]{1,0:T(8,128)} custom-call(f32[2048,2048]{1,0:T(8,128)} %v_hbm.1, f32[16,2,64,64]{3,2,1,0:T(8,128)} %bitcast.3, f32[64,8192]{1,0:T(8,128)} %bitcast.2), custom_call_target="tpu_custom_call" | custom-call | tf_op jit(solution)/shard_map/pallas_call | solution.py:606
  282.7 3.0 %copy.5 = f32[2048,256]{1,0:T(8,128)} copy(f32[2048,256]{1,0:T(8,128)} %shard_map.37) | data formatting | bytes 4194304

commit v6 on v5

--- a/solution.py
+++ b/solution.py
@@ -9,6 +9,9 @@
 BF16 = jnp.bfloat16
 MESH = pl.DeviceIdType.MESH
 TILE = 256
+LANE = 128
+WIDE = 64
+PAIR = range(2)
 AHEAD = 8
 GATHER = 8
 
@@ -66,11 +69,11 @@
         pl.semaphore_wait(barrier, 6)
 
         def v_src(hh):
-            n = 128 * (blocks - hh)
-            return v_hbm.at[pl.ds(rows - n, n), pl.ds(hh * 128, 128)]
+            n = LANE * (blocks - hh)
+            return v_hbm.at[pl.ds(rows - n, n), pl.ds(hh * LANE, LANE)]
 
         def v_rows(base, hh):
-            return vbuf.at[pl.ds(base + 128 * (hh % 2), 128 * (blocks - hh)), :]
+            return vbuf.at[pl.ds(base + LANE * (hh % 2), LANE * (blocks - hh)), :]
 
         def v_dst(rel, hh):
             return v_rows(area * (rel - 1) + TILE * tiles_before(hh), hh)
@@ -90,8 +93,8 @@
         def clear_v():
             for rel in range(3):
                 for hh in range(1, blocks, 2):
-                    vbuf[pl.ds(area * rel + TILE * tiles_before(hh), 128), :] = jnp.zeros((128, 128), F32)
-            vbuf[pl.ds(3 * area + rows, 128), :] = jnp.zeros((128, 128), F32)
+                    vbuf[pl.ds(area * rel + TILE * tiles_before(hh), LANE), :] = jnp.zeros((LANE, LANE), F32)
+            vbuf[pl.ds(3 * area + rows, LANE), :] = jnp.zeros((LANE, LANE), F32)
 
         def v_arrive(rel, hh):
             return remote(v_src(hh), v_dst(rel, hh), vx_s.at[hh], v_r.at[rel - 1, hh], dev_x)
@@ -127,10 +130,10 @@
                 t_arrive(slot, hh).wait_recv()
 
         def z_src(to, t, part):
-            return z_hbm.at[:, pl.ds(pl.multiple_of(rows * to + TILE * t + 128 * part, 128), 128)]
+            return z_hbm.at[:, pl.ds(pl.multiple_of(rows * to + TILE * t + LANE * part, LANE), LANE)]
 
         def z_dst(src_r, t, part):
-            return xt.at[t, pl.ds(pl.multiple_of(64 * src_r, 64), 64), pl.ds(128 * part, 128)]
+            return xt.at[t, pl.ds(pl.multiple_of(WIDE * src_r, WIDE), WIDE), pl.ds(LANE * part, LANE)]
 
         def z_copies(t, part):
             return [remote(z_src(dev[0], t, part), z_dst(r, t, part), z_s.at[i, t, part], z_r.at[r, t, part], dev)
@@ -145,7 +148,7 @@
             z_loc(t, part).start()
 
         def collect_z(t):
-            for part in range(2):
+            for part in PAIR:
                 z_loc(t, part).wait()
                 for src_r in (ry, rz, rd):
                     dst = z_dst(src_r, t, part)
@@ -155,11 +158,11 @@
             return (dev_y, dev_z) if half == 0 else (dev_z, dev_y)
 
         def w_p1(p, half):
-            s = pl.ds(128 * half, 128)
+            s = pl.ds(LANE * half, LANE)
             return remote(wacc.at[p, s], r1.at[p, s], p1_s.at[p, half], p1_r.at[p, half], steps(half)[0])
 
         def w_p2(p, half):
-            s = pl.ds(128 * half, 128)
+            s = pl.ds(LANE * half, LANE)
             return remote(ws.at[p, s], r2.at[p, s], p2_s.at[p, half], p2_r.at[p, half], steps(half)[1])
 
         def g_place(f):
@@ -171,7 +174,7 @@
 
         def w_kept(f, other=0):
             k1 = r % 2 if f == 0 else r // 2
-            return g_rows(128 * f + 64 * (k1 + other * (1 - 2 * k1)), 64)
+            return g_rows(LANE * f + WIDE * (k1 + other * (1 - 2 * k1)), WIDE)
 
         def w_e1(p, f):
             s = w_kept(f, 1)
@@ -186,17 +189,17 @@
             return remote(wacc.at[p, s], wacc.at[p, s], w_s.at[2, p, f], w_r.at[2, p, f], steps(f)[0])
 
         def w_act1(p):
-            for f in range(2):
+            for f in PAIR:
                 w_e1(p, f).wait()
-            for f in range(2):
+            for f in PAIR:
                 s = w_kept(f)
                 ws[p, s] = wacc[p, s] + r1[p, s]
                 w_e2(p, f).start()
 
         def w_act2(p):
-            for f in range(2):
+            for f in PAIR:
                 w_e2(p, f).wait()
-            for f in range(2):
+            for f in PAIR:
                 s = w_kept(f)
                 wacc[p, s] = ws[p, s] + r2[p, s]
                 w_e3(p, f).start()
@@ -210,10 +213,10 @@
             return remote(gacc.at[par, s], gr2.at[par, s], g_s.at[1, par, f], g_r.at[1, par, f], steps(f)[1])
 
         def act_p2(par):
-            for f in range(2):
+            for f in PAIR:
                 g_p1(par, f).wait()
             gacc[par] = gacc[par] + gr1[par]
-            for f in range(2):
+            for f in PAIR:
                 g_p2(par, f).start()
 
         def g_rs1(par, f):
@@ -237,16 +240,16 @@
             return remote(gf.at[par, s], gf.at[par, s], g_s.at[3, par, f], g_r.at[3, par, f], steps(f)[0])
 
         def act_rs2(par):
-            for f in range(2):
+            for f in PAIR:
                 g_rs1(par, f).wait()
-            for f in range(2):
+            for f in PAIR:
                 base, k1, _ = g_place(f)
                 s = g_rows(base + 112 * k1, 112)
                 gacc[par, s] = gacc[par, s] + gr1[par, s]
                 g_rs2(par, f).start()
 
         def act_ag2(par):
-            for f in range(2):
+            for f in PAIR:
                 base, k1, k2 = g_place(f)
                 g_rs2(par, f).wait()
                 s = g_rows(base + 112 * k1 + 56 * k2, 56)
@@ -254,7 +257,7 @@
                 g_ag2(par, f).start()
 
         def act_ag1(par):
-            for f in range(2):
+            for f in PAIR:
                 g_ag2(par, f).wait()
                 g_ag1(par, f).start()
 
@@ -287,15 +290,15 @@
 
             def one(t, _):
                 d = pl.ds(pl.multiple_of(TILE * t, TILE), TILE)
-                for i in range(2):
+                for i in PAIR:
                     a = vbuf[pl.ds(pl.multiple_of(bases[2 * i] + TILE * t, TILE), TILE), :]
                     b = vbuf[pl.ds(pl.multiple_of(bases[2 * i + 1] + TILE * t, TILE), TILE), :]
-                    low = lax.broadcasted_iota(jnp.int32, a.shape, 1) < 64
-                    ar, br = pltpu.roll(a, 64, 1), pltpu.roll(b, 64, 1)
+                    low = lax.broadcasted_iota(jnp.int32, a.shape, 1) < WIDE
+                    ar, br = pltpu.roll(a, WIDE, 1), pltpu.roll(b, WIDE, 1)
                     for k, part in enumerate(split(jnp.where(low, a, br))):
-                        vp[slot, k, d, 128 * i:128 * i + 128] = part
+                        vp[slot, k, d, LANE * i:LANE * i + LANE] = part
                     for k, part in enumerate(split(jnp.where(low, ar, b))):
-                        vp[slot, k, d, 256 + 128 * i:256 + 128 * i + 128] = part
+                        vp[slot, k, d, TILE + LANE * i:TILE + LANE * i + LANE] = part
                 return 0
             lax.fori_loop(0, tiles_of(h), one, 0)
 
@@ -305,27 +308,27 @@
 
         def gram(h, slot):
             gkk[...] = jnp.zeros_like(gkk)
-            mine = pl.ds(pl.multiple_of(256 * core, 256), 256)
-            half = pl.ds(pl.multiple_of(128 * core, 128), 128)
+            mine = pl.ds(pl.multiple_of(TILE * core, TILE), TILE)
+            half = pl.ds(pl.multiple_of(LANE * core, LANE), LANE)
 
             def one(t, n):
                 own = [parts(slot, t + u, mine) for u in range(n)]
-                gkk[0:256, :] += dot6([(a, a) for a in own], 0, 0)
-                gkk[256:384, :] += dot6([(parts(slot, t + u, half), parts(slot, t + u, pl.ds(256, 256)))
+                gkk[0:TILE, :] += dot6([(a, a) for a in own], 0, 0)
+                gkk[TILE:384, :] += dot6([(parts(slot, t + u, half), parts(slot, t + u, pl.ds(TILE, TILE)))
                                          for u in range(n)], 0, 0)
             over_tiles(tiles_of(h), one)
 
         def send_g(par, first=g_rs1):
-            gacc[par, 0:128, :] = gkk[256:384, 0:128]
-            gacc[par, 128:256, :] = gkk[256:384, 128:256]
-            gacc[par, 256:384, :] = gkk[0:128, 128:256]
-            gacc[par, 384:448, 0:64] = gkk[0:64, 64:128]
-            gacc[par, 384:448, 64:128] = gkk[128:192, 192:256]
-            for f in range(2):
+            gacc[par, 0:LANE, :] = gkk[TILE:384, 0:LANE]
+            gacc[par, LANE:TILE, :] = gkk[TILE:384, LANE:TILE]
+            gacc[par, TILE:384, :] = gkk[0:LANE, LANE:TILE]
+            gacc[par, 384:448, 0:WIDE] = gkk[0:WIDE, WIDE:LANE]
+            gacc[par, 384:448, WIDE:LANE] = gkk[LANE:192, 192:TILE]
+            for f in PAIR:
                 first(par, f).start()
 
         def rows_of(k):
-            return pl.ds(pl.multiple_of(128 * k, 128), 128)
+            return pl.ds(pl.multiple_of(LANE * k, LANE), LANE)
 
         def share(slot, k):
             return (remote(tbuf.at[slot, k], tbuf.at[slot, k], d_s.at[slot, 0], d_r.at[slot, 0], dev_sib),
@@ -334,32 +337,32 @@
         def merge(h, slot):
             @pl.when(h >= last - 1)
             def _():
-                for f in range(2):
+                for f in PAIR:
                     g_p2(slot, f).wait()
                 gf[slot] = gacc[slot] + gr2[slot]
 
             @pl.when(h < last - 1)
             def _():
-                for f in range(2):
+                for f in PAIR:
                     g_ag1(slot, f).wait()
             g = gf[slot]
-            gab[slot, rows_of(core), 0:128] = g[0:128]
-            gab[slot, rows_of(core), 128:256] = g[128:256]
-            zero = jnp.zeros((64, 64), F32)
+            gab[slot, rows_of(core), 0:LANE] = g[0:LANE]
+            gab[slot, rows_of(core), LANE:TILE] = g[LANE:TILE]
+            zero = jnp.zeros((WIDE, WIDE), F32)
 
             def diag(a, b):
                 return jnp.concatenate([jnp.concatenate([a, zero], 1), jnp.concatenate([zero, b], 1)], 0)
             t0, t1, t2, t3 = (tall[i, h] for i in range(4))
             low = g[384:448]
-            off = dot(diag(low[:, 0:64], low[:, 64:128]), diag(t1, t3), 1, 0)
+            off = dot(diag(low[:, 0:WIDE], low[:, WIDE:LANE]), diag(t1, t3), 1, 0)
             off = -dot(diag(t0, t2), off, 1, 0)
-            ta = jnp.concatenate([jnp.concatenate([t0, off[0:64, 0:64]], 1), jnp.concatenate([zero, t1], 1)], 0)
-            tb = jnp.concatenate([jnp.concatenate([t2, off[64:128, 64:128]], 1), jnp.concatenate([zero, t3], 1)], 0)
-            cross = -dot(ta, dot(g[256:384], tb, 1, 0), 1, 0)
-            tbuf[slot, core, 0:128, 0:128] = ta
-            tbuf[slot, core, 0:128, 128:256] = cross
-            tbuf[slot, core, 128:256, 0:128] = jnp.zeros((128, 128), F32)
-            tbuf[slot, core, 128:256, 128:256] = tb
+            ta = jnp.concatenate([jnp.concatenate([t0, off[0:WIDE, 0:WIDE]], 1), jnp.concatenate([zero, t1], 1)], 0)
+            tb = jnp.concatenate([jnp.concatenate([t2, off[WIDE:LANE, WIDE:LANE]], 1), jnp.concatenate([zero, t3], 1)], 0)
+            cross = -dot(ta, dot(g[TILE:384], tb, 1, 0), 1, 0)
+            tbuf[slot, core, 0:LANE, 0:LANE] = ta
+            tbuf[slot, core, 0:LANE, LANE:TILE] = cross
+            tbuf[slot, core, LANE:TILE, 0:LANE] = jnp.zeros((LANE, LANE), F32)
+            tbuf[slot, core, LANE:TILE, LANE:TILE] = tb
             for cp in share(slot, core):
                 cp.start()
 
@@ -369,8 +372,8 @@
             for cp in share(slot, 1 - core):
                 cp.wait_recv()
             tb = tbuf[slot, 1]
-            nbuf[0:256, :] = tb
-            nbuf[256:512, :] = dot(dot(tbuf[slot, 0], gab[slot], 1, 0), tb, 1, 0)
+            nbuf[0:TILE, :] = tb
+            nbuf[TILE:512, :] = dot(dot(tbuf[slot, 0], gab[slot], 1, 0), tb, 1, 0)
 
         def gathered(h):
             return jnp.logical_and(h >= GATHER, h < last)
@@ -383,8 +386,8 @@
 
             def group(i, _):
                 p = 1 - i
-                wacc[p] = jnp.zeros((256, 256), F32)
-                lanes = pl.ds(pl.multiple_of(256 * p, 256), 256)
+                wacc[p] = jnp.zeros((TILE, TILE), F32)
+                lanes = pl.ds(pl.multiple_of(TILE * p, TILE), TILE)
 
                 def one(t, n):
                     wacc[p] += dot6([(split(xt[t0 + t + u]), parts(slot, t + u, lanes)) for u in range(n)], 1, 0)
@@ -392,35 +395,35 @@
                 if run is whole:
                     @pl.when(gathered(h))
                     def _():
-                        for f in range(2):
+                        for f in PAIR:
                             w_e1(p, f).start()
 
                     @pl.when(h < GATHER)
                     def _():
-                        for half in range(2):
+                        for half in PAIR:
                             w_p1(p, half).start()
                 else:
-                    for half in range(2):
+                    for half in PAIR:
                         w_p1(p, half).start()
                 return 0
             lax.fori_loop(0, 2, group, 0)
 
         def act_w(p):
-            for half in range(2):
+            for half in PAIR:
                 w_p1(p, half).wait()
             ws[p] = wacc[p] + r1[p]
-            for half in range(2):
+            for half in PAIR:
                 w_p2(p, half).start()
 
         def reduced(h, p):
             @pl.when(gathered(h))
             def _():
-                for f in range(2):
+                for f in PAIR:
                     w_e3(p, f).wait()
 
             @pl.when(pairwise(h))
             def _():
-                for half in range(2):
+                for half in PAIR:
                     w_p2(p, half).wait()
                 wacc[p] = ws[p] + r2[p]
             return wacc[p]
@@ -432,7 +435,7 @@
 
             def one(t, n):
                 for u in range(n):
-                    xt[t0 + t + u] += dot6([(tuple(yp[k] for k in range(3)), parts(slot, t + u, pl.ds(256 * p, 256)))], 1, 1)
+                    xt[t0 + t + u] += dot6([(tuple(yp[k] for k in range(3)), parts(slot, t + u, pl.ds(TILE * p, TILE)))], 1, 1)
             whole(tiles_of(h), one)
 
         def ready(h, slot):
@@ -448,12 +451,12 @@
         top = rows // TILE - 1
         issue_v(last)
         v_loc(last).start()
-        for part in range(2):
+        for part in PAIR:
             issue_z(top, part)
         for hh in range(last - 1, last - AHEAD, -1):
             issue_v(hh)
         v_loc(last - 1).start()
-        for part in range(2):
+        for part in PAIR:
             issue_z(top - 1, part)
         clear_v()
         forward_v(last)
@@ -545,14 +548,9 @@
             def _():
                 send_g(slot)
 
-            @pl.when(h == last)
-            def _():
-                for part in range(2):
-                    issue_z(top - 2, part)
-
-            @pl.when(jnp.logical_and(h <= last - 2, h >= last - top + 1))
-            def _():
-                for part in range(2):
+            @pl.when(jnp.logical_and(h < last, h >= last - top + 1))
+            def _():
+                for part in PAIR:
                     issue_z(h - (last - top + 1), part)
             for hh in range(blocks - 3):
                 @pl.when(h - 3 == hh)
@@ -560,8 +558,8 @@
                     forward_v(hh)
             factor(slot)
             yb = dot(reduced(h, 1), nbuf[...], 1, 1)
-            ws[1] = yb[:, 256:512]
-            update(h, vslot, 1, yb[:, 0:256])
+            ws[1] = yb[:, TILE:512]
+            update(h, vslot, 1, yb[:, 0:TILE])
             ya = dot(reduced(h, 0), tbuf[slot, 0], 1, 1) - ws[1]
             update(h, vslot, 0, ya)
 
@@ -571,16 +569,8 @@
             return 0
 
         lax.fori_loop(0, blocks, block_step, 0)
-        stages = [buf.at[k] for buf in (wacc, r1, ws, r2) for k in range(2)]
-        outs = []
-        for t in range(rows // TILE):
-            if t >= len(stages):
-                outs[t - len(stages)].wait()
-            stages[t % len(stages)][...] = xt[t].T
-            outs.append(pltpu.make_async_copy(stages[t % len(stages)], o_hbm.at[pl.ds(TILE * t, TILE), :], o_s.at[t]))
-            outs[t].start()
-        for cp in outs[-len(stages):]:
-            cp.wait()
+        out = pltpu.make_async_copy(xt, o_hbm, o_s)
+        out.start()
         for hh in range(blocks):
             v_x(hh).wait_send()
             v_sib(hh).wait_send()
@@ -588,9 +578,10 @@
             for cp in t_copies(hh):
                 cp.wait_send()
         for t in range(rows // TILE):
-            for part in range(2):
+            for part in PAIR:
                 for cp in z_copies(t, part):
                     cp.wait_send()
+        out.wait()
 
     return body
 
@@ -598,41 +589,43 @@
 def solution(mesh):
     def local(v_loc, t_loc, z_loc):
         rows, cols = v_loc.shape
-        blocks = cols // 128
-        t_loc = t_loc.reshape(blocks, 2, 64, 64)
+        blocks = cols // LANE
+        t_loc = t_loc.reshape(blocks, 2, WIDE, WIDE)
         tiles = ((blocks + 1) // 2) * ((blocks + 2) // 2)
         dma = pltpu.SemaphoreType.DMA
         hbm = pl.BlockSpec(memory_space=pl.ANY)
-        return pl.pallas_call(
+        xt = pl.pallas_call(
             make_kernel(rows, blocks),
-            out_shape=jax.ShapeDtypeStruct((rows, 256), F32),
+            out_shape=jax.ShapeDtypeStruct((rows // TILE, TILE, TILE), F32),
             in_specs=[hbm] * 3,
             out_specs=hbm,
             scratch_shapes=[
-                pltpu.VMEM((3 * TILE * tiles + 2 * rows, 128), F32),
+                pltpu.VMEM((3 * TILE * tiles + 2 * rows, LANE), F32),
                 pltpu.VMEM((3, 3, rows, 512), BF16),
-                pltpu.VMEM((4, blocks, 64, 64), F32),
-                pltpu.VMEM((rows // TILE, 256, TILE), F32),
-                pltpu.VMEM((2, 256, 256), F32), pltpu.VMEM((2, 256, 256), F32),
-                pltpu.VMEM((2, 256, 256), F32), pltpu.VMEM((2, 256, 256), F32),
-                pltpu.VMEM((3, 256, 256), BF16),
-                pltpu.VMEM((384, 256), F32),
-                pltpu.VMEM((2, 448, 128), F32), pltpu.VMEM((2, 448, 128), F32),
-                pltpu.VMEM((2, 448, 128), F32), pltpu.VMEM((2, 448, 128), F32),
-                pltpu.VMEM((2, 2, 256, 256), F32),
-                pltpu.VMEM((2, 256, 256), F32),
-                pltpu.VMEM((512, 256), F32),
+                pltpu.VMEM((4, blocks, WIDE, WIDE), F32),
+                pltpu.VMEM((rows // TILE, TILE, TILE), F32),
+                pltpu.VMEM((2, TILE, TILE), F32), pltpu.VMEM((2, TILE, TILE), F32),
+                pltpu.VMEM((2, TILE, TILE), F32), pltpu.VMEM((2, TILE, TILE), F32),
+                pltpu.VMEM((3, TILE, TILE), BF16),
+                pltpu.VMEM((384, TILE), F32),
+                pltpu.VMEM((2, 448, LANE), F32), pltpu.VMEM((2, 448, LANE), F32),
+                pltpu.VMEM((2, 448, LANE), F32), pltpu.VMEM((2, 448, LANE), F32),
+                pltpu.VMEM((2, 2, TILE, TILE), F32),
+                pltpu.VMEM((2, TILE, TILE), F32),
+                pltpu.VMEM((512, TILE), F32),
                 dma((blocks,)), dma((blocks,)), dma((blocks,)), dma((blocks,)), dma((3, blocks)),
                 dma((blocks,)), dma((blocks,)), dma((blocks,)), dma((blocks,)), dma((4, blocks)),
                 dma((3, rows // TILE, 2)), dma((rows // TILE, 2)), dma((4, rows // TILE, 2)),
                 dma((2, 2)), dma((2, 2)), dma((2, 2)), dma((2, 2)),
                 dma((4, 2, 2)), dma((4, 2, 2)), dma((4, 2, 2)), dma((4, 2, 2)),
-                dma((2, 2)), dma((2, 2)), dma((rows // TILE,)),
+                dma((2, 2)), dma((2, 2)), dma,
             ],
             compiler_params=pltpu.CompilerParams(collective_id=0, has_side_effects=True,
                                                  vmem_limit_bytes=67043328),
         )(v_loc, t_loc, z_loc.T)
 
+        return xt.transpose(0, 2, 1).reshape(rows, TILE)
+
     return jax.shard_map(local, mesh=mesh,
                          in_specs=(P('row', 'col'), P('col', None, None), P(None, ('col', 'row'))),
                          out_specs=P('row', 'col'), check_vma=False)

time: 286 us -> 285 us (level)
    unnamed x1 -> x0, local copies, waits for them, and re-layouts: 3.05 us -> none
    transpose x0 -> x1, local copies, waits for them, and re-layouts: none -> 2.88 us  [local(): return xt.transpose(0, 2, 1).reshape(rows, TILE)]
where the time goes in v6:
time: 285 us
  Pallas kernels  282 us (99%)
  local copies, waits for them, and re-layouts  2.88 us (1%)
    pallas_call x1, Pallas kernels, local(): pl.pallas_call(make_kernel(rows, blocks), out_shape=jax.ShapeDtypeStruct(...  282 us

profile of v6, /device:TPU:0, one launch (start us, length us, event | category | flops | bytes accessed | tf_op | source)
XLA Modules:
  0.0 284.8 jit_solution(10403281830178963026)
XLA Ops:
  0.0 281.9 %shard_map.37 = f32[8,256,256]{2,1,0:T(8,128)} custom-call(f32[2048,2048]{1,0:T(8,128)} %v_hbm.1, f32[16,2,64,64]{3,2,1,0:T(8,128)} %bitcast.6, f32[64,8192]{1,0:T(8,128)} %bitcast.5), custom_call_target="tpu_custom_call" | custom-call | tf_op jit(solution)/shard_map/pallas_call | solution.py:597
  281.9 2.9 %copy.4 = f32[8,256,256]{2,1,0:T(8,128)} copy(f32[8,256,256]{1,2,0:T(8,128)} %bitcast.4) | data formatting | bytes 4194304 | tf_op jit(solution)/shard_map/transpose | solution.py:627

commit v7 on v6

--- a/solution.py
+++ b/solution.py
@@ -14,6 +14,7 @@
 PAIR = range(2)
 AHEAD = 8
 GATHER = 8
+EARLY = 4
 
 
 def dot(a, b, ca, cb):
@@ -281,7 +282,7 @@
                 def _():
                     fn(0, k)
 
-        def prepare(h, slot):
+        def prepare(h, slot, start, stop):
             bases = []
             for i in range(4):
                 rel = ((c // 2 + i // 2) % 2) * 2 + (c + i) % 2
@@ -300,22 +301,30 @@
                     for k, part in enumerate(split(jnp.where(low, ar, b))):
                         vp[slot, k, d, TILE + LANE * i:TILE + LANE * i + LANE] = part
                 return 0
-            lax.fori_loop(0, tiles_of(h), one, 0)
+            lax.fori_loop(start, stop, one, 0)
 
         def parts(slot, t, lanes):
             s = pl.ds(pl.multiple_of(TILE * t, TILE), TILE)
             return tuple(vp[slot, k, s, lanes] for k in range(3))
 
-        def gram(h, slot):
-            gkk[...] = jnp.zeros_like(gkk)
+        top3 = LANE + WIDE
+
+        def gram_own(h, slot):
+            gkk[0:top3, :] = jnp.zeros((top3, TILE), F32)
             mine = pl.ds(pl.multiple_of(TILE * core, TILE), TILE)
-            half = pl.ds(pl.multiple_of(LANE * core, LANE), LANE)
 
             def one(t, n):
                 own = [parts(slot, t + u, mine) for u in range(n)]
-                gkk[0:TILE, :] += dot6([(a, a) for a in own], 0, 0)
-                gkk[TILE:384, :] += dot6([(parts(slot, t + u, half), parts(slot, t + u, pl.ds(TILE, TILE)))
-                                         for u in range(n)], 0, 0)
+                gkk[0:top3, :] += dot6([(tuple(x[:, 0:top3] for x in a), a) for a in own], 0, 0)
+            over_tiles(tiles_of(h), one)
+
+        def gram_cross(h, slot):
+            gkk[TILE:TILE + LANE, :] = jnp.zeros((LANE, TILE), F32)
+            half = pl.ds(pl.multiple_of(LANE * core, LANE), LANE)
+
+            def one(t, n):
+                gkk[TILE:TILE + LANE, :] += dot6([(parts(slot, t + u, half), parts(slot, t + u, pl.ds(TILE, TILE)))
+                                                  for u in range(n)], 0, 0)
             over_tiles(tiles_of(h), one)
 
         def send_g(par, first=g_rs1):
@@ -335,13 +344,13 @@
                     remote(gab.at[slot, rows_of(k)], gab.at[slot, rows_of(k)], d_s.at[slot, 1], d_r.at[slot, 1], dev_sib))
 
         def merge(h, slot):
-            @pl.when(h >= last - 1)
+            @pl.when(jnp.logical_or(h >= last - 1, h == 0))
             def _():
                 for f in PAIR:
                     g_p2(slot, f).wait()
                 gf[slot] = gacc[slot] + gr2[slot]
 
-            @pl.when(h < last - 1)
+            @pl.when(jnp.logical_and(h > 0, h < last - 1))
             def _():
                 for f in PAIR:
                     g_ag1(slot, f).wait()
@@ -440,13 +449,9 @@
 
         def ready(h, slot):
             collect_v(h)
-            prepare(h, slot)
-            gram(h, slot)
-
-        def ready(h, slot):
-            collect_v(h)
-            prepare(h, slot)
-            gram(h, slot)
+            prepare(h, slot, 0, tiles_of(h))
+            gram_own(h, slot)
+            gram_cross(h, slot)
 
         top = rows // TILE - 1
         issue_v(last)
@@ -473,6 +478,11 @@
         send_g((last - 1) % 2, g_p1)
         forward_v(last - 2)
 
+        def pick(k, n, fn):
+            @pl.when(k >= 0)
+            def _():
+                lax.switch(k, [lambda hh=hh: fn(hh) for hh in range(n)])
+
         def block_step(i, _):
             h = last - i
             slot = h % 2
@@ -486,76 +496,87 @@
             def _():
                 product(h, vslot, whole)
 
+            @pl.when(pairwise(h))
+            def _():
+                merge(h, slot)
+
+            @pl.when(h == last - 1)
+            def _():
+                act_p2(slot)
+
+            @pl.when(jnp.logical_and(h > 1, h < GATHER))
+            def _():
+                act_rs2(1 - slot)
+            pick(h - AHEAD, blocks - AHEAD, issue_v)
+
+            nb = h - 2 + (blocks + 1 - h) // blocks
+            active = jnp.logical_or(h > 2, h == 1)
+
+            @pl.when(active)
+            def _():
+                pick(nb, blocks - 2, collect_v)
+
+            n2 = tiles_of(nb)
+            part = EARLY * n2 // 8
+            cut = part + (n2 - part) * ((h + blocks - GATHER) // blocks)
+
+            @pl.when(active)
+            def _():
+                prepare(nb, nb % 3, 0, cut)
+
+            @pl.when(h < GATHER)
+            def _():
+                act_w(1)
+
+            @pl.when(jnp.logical_and(active, h < GATHER))
+            def _():
+                prepare(nb, nb % 3, cut, n2)
+
+            @pl.when(active)
+            def _():
+                gram_own(nb, nb % 3)
+
             @pl.when(gathered(h))
             def _():
                 w_act1(1)
+
+            @pl.when(h < GATHER)
+            def _():
+                act_w(0)
+
+            @pl.when(active)
+            def _():
+                gram_cross(nb, nb % 3)
+            pick(h - 3, blocks - 3, lambda hh: v_loc(hh).start())
+
+            @pl.when(gathered(h))
+            def _():
                 w_act1(0)
-
-            @pl.when(h != last - 1)
-            def _():
                 merge(h, slot)
-
-            @pl.when(h == last - 1)
-            def _():
-                act_p2(slot)
-
-            @pl.when(jnp.logical_and(h > 0, h < last))
-            def _():
                 act_rs2(1 - slot)
-            for hh in range(blocks - AHEAD):
-                @pl.when(h == hh + AHEAD)
-                def _():
-                    issue_v(hh)
-            for hh in range(blocks - 2):
-                @pl.when(h - 2 == hh)
-                def _():
-                    collect_v(hh)
-
-            @pl.when(h > 1)
-            def _():
-                prepare(h - 2, (h - 2) % 3)
-            for hh in range(blocks - 3):
-                @pl.when(h - 3 == hh)
-                def _():
-                    v_loc(hh).start()
-
-            @pl.when(h < GATHER)
-            def _():
-                act_w(1)
-
-            @pl.when(gathered(h))
-            def _():
                 w_act2(1)
                 w_act2(0)
 
-            @pl.when(h > 1)
-            def _():
-                gram(h - 2, (h - 2) % 3)
-
-            @pl.when(h < GATHER)
-            def _():
-                act_w(0)
-
-            @pl.when(h == last - 1)
-            def _():
-                merge(h, slot)
-
-            @pl.when(jnp.logical_and(h > 0, h < last))
+            @pl.when(jnp.logical_and(h > 1, h < last))
             def _():
                 act_ag2(1 - slot)
 
-            @pl.when(h > 1)
+            @pl.when(h > 2)
             def _():
                 send_g(slot)
+
+            @pl.when(h == 1)
+            def _():
+                send_g(0, g_p1)
 
             @pl.when(jnp.logical_and(h < last, h >= last - top + 1))
             def _():
                 for part in PAIR:
                     issue_z(h - (last - top + 1), part)
-            for hh in range(blocks - 3):
-                @pl.when(h - 3 == hh)
-                def _():
-                    forward_v(hh)
+
+            @pl.when(jnp.logical_or(h > 3, h == 2))
+            def _():
+                pick(h - 3 + (blocks + 2 - h) // blocks, blocks - 3, forward_v)
             factor(slot)
             yb = dot(reduced(h, 1), nbuf[...], 1, 1)
             ws[1] = yb[:, TILE:512]
@@ -563,9 +584,13 @@
             ya = dot(reduced(h, 0), tbuf[slot, 0], 1, 1) - ws[1]
             update(h, vslot, 0, ya)
 
-            @pl.when(jnp.logical_and(h > 0, h < last))
+            @pl.when(jnp.logical_and(h > 1, h < last))
             def _():
                 act_ag1(1 - slot)
+
+            @pl.when(h == 1)
+            def _():
+                act_p2(0)
             return 0
 
         lax.fori_loop(0, blocks, block_step, 0)

time: 285 us -> 281 us (0.986)
  Pallas kernels: 282 us -> 278 us
    pallas_call x1, Pallas kernels: 282 us -> 278 us  [local(): pl.pallas_call(make_kernel(rows, blocks), out_shape=jax.ShapeDtypeStruct(...]
where the time goes in v7:
time: 281 us
  Pallas kernels  278 us (99%)
  local copies, waits for them, and re-layouts  2.88 us (1%)
    pallas_call x1, Pallas kernels, local(): pl.pallas_call(make_kernel(rows, blocks), out_shape=jax.ShapeDtypeStruct(...  278 us

profile of v7, /device:TPU:0, one launch (start us, length us, event | category | flops | bytes accessed | tf_op | source)
XLA Modules:
  0.0 280.8 jit_solution(7864464633099591503)
XLA Ops:
  0.0 277.9 %shard_map.37 = f32[8,256,256]{2,1,0:T(8,128)} custom-call(f32[2048,2048]{1,0:T(8,128)} %v_hbm.1, f32[16,2,64,64]{3,2,1,0:T(8,128)} %bitcast.6, f32[64,8192]{1,0:T(8,128)} %bitcast.5), custom_call_target="tpu_custom_call" | custom-call | tf_op jit(solution)/shard_map/pallas_call | solution.py:622
  277.9 2.9 %copy.4 = f32[8,256,256]{2,1,0:T(8,128)} copy(f32[8,256,256]{1,2,0:T(8,128)} %bitcast.4) | data formatting | bytes 4194304 | tf_op jit(solution)/shard_map/transpose | solution.py:652

commit v8 on v7

--- a/solution.py
+++ b/solution.py
@@ -496,7 +496,7 @@
             def _():
                 product(h, vslot, whole)
 
-            @pl.when(pairwise(h))
+            @pl.when(jnp.logical_and(pairwise(h), h > 0))
             def _():
                 merge(h, slot)
 
@@ -527,6 +527,10 @@
             @pl.when(h < GATHER)
             def _():
                 act_w(1)
+
+            @pl.when(h == 0)
+            def _():
+                merge(h, slot)
 
             @pl.when(jnp.logical_and(active, h < GATHER))
             def _():

time: 281 us -> 281 us (level)
  no operation moved by 1% of the time
where the time goes in v8:
time: 281 us
  Pallas kernels  278 us (99%)
  local copies, waits for them, and re-layouts  2.88 us (1%)
    pallas_call x1, Pallas kernels, local(): pl.pallas_call(make_kernel(rows, blocks), out_shape=jax.ShapeDtypeStruct(...  278 us

profile of v8, /device:TPU:0, one launch (start us, length us, event | category | flops | bytes accessed | tf_op | source)
XLA Modules:
  0.0 280.8 jit_solution(123065463323784044)
XLA Ops:
  0.0 277.9 %shard_map.37 = f32[8,256,256]{2,1,0:T(8,128)} custom-call(f32[2048,2048]{1,0:T(8,128)} %v_hbm.1, f32[16,2,64,64]{3,2,1,0:T(8,128)} %bitcast.6, f32[64,8192]{1,0:T(8,128)} %bitcast.5), custom_call_target="tpu_custom_call" | custom-call | tf_op jit(solution)/shard_map/pallas_call | solution.py:626
  277.9 2.9 %copy.4 = f32[8,256,256]{2,1,0:T(8,128)} copy(f32[8,256,256]{1,2,0:T(8,128)} %bitcast.4) | data formatting | bytes 4194304 | tf_op jit(solution)/shard_map/transpose | solution.py:656
